TPU v7x, 8 devices: a whole 2x2x1 slice. The times are simulated.
8 devices in a mesh: dp: 1 (over z), tp: 8 (over y, x, core).
Axes of the slice: x: 2, y: 2, z: 1, core: 2. Of those that a mesh axis runs over, the one named last changes fastest.
Arguments:
- x_in: bfloat16 [8, 64, 4096], P('dp', 'tp')
- seg_pos: int32 [8, 64], P('dp')
- conv_state: bfloat16 [2, 8, 3, 4096], P(None, 'dp', None, 'tp')
- lru_state: float32 [2, 8, 4096], P(None, 'dp', 'tp')
- k_cache: bfloat16 [8, 2048, 256], P('dp')
- v_cache: bfloat16 [8, 2048, 256], P('dp')
- slot_pos: int32 [8, 2048], P('dp')
- norm_scale: bfloat16 [6, 4096], replicated
- w_x: bfloat16 [2, 4096, 4096], P(None, None, 'tp')
- b_x: bfloat16 [2, 4096], P(None, 'tp')
- w_y: bfloat16 [2, 4096, 4096], P(None, None, 'tp')
- b_y: bfloat16 [2, 4096], P(None, 'tp')
- conv_w: bfloat16 [2, 4, 4096], P(None, None, 'tp')
- conv_b: bfloat16 [2, 4096], P(None, 'tp')
- w_a: bfloat16 [2, 16, 256, 256], P(None, 'tp')
- b_a: bfloat16 [2, 4096], P(None, 'tp')
- w_i: bfloat16 [2, 16, 256, 256], P(None, 'tp')
- b_i: bfloat16 [2, 4096], P(None, 'tp')
- a_param: float32 [2, 4096], P(None, 'tp')
- w_out: bfloat16 [2, 4096, 4096], P(None, 'tp')
- b_out: bfloat16 [2, 4096], replicated
- w_q: bfloat16 [4096, 4096], P(None, 'tp')
- w_k: bfloat16 [4096, 256], replicated
- w_v: bfloat16 [4096, 256], replicated
- w_o: bfloat16 [4096, 4096], P('tp')
- b_o: bfloat16 [4096], replicated
- w_1: bfloat16 [3, 4096, 12288], P(None, None, 'tp')
- b_1: bfloat16 [3, 12288], P(None, 'tp')
- w_2: bfloat16 [3, 4096, 12288], P(None, None, 'tp')
- b_2: bfloat16 [3, 12288], P(None, 'tp')
- w_d: bfloat16 [3, 12288, 4096], P(None, 'tp')
- b_d: bfloat16 [3, 4096], replicated
Outputs:
- output 1: bfloat16 [8, 64, 4096], P('dp', 'tp')
- output 2: bfloat16 [2, 8, 3, 4096], P(None, 'dp', None, 'tp')
- output 3: float32 [2, 8, 4096], P(None, 'dp', 'tp')
- output 4: bfloat16 [8, 2048, 256], P('dp')
- output 5: bfloat16 [8, 2048, 256], P('dp')
- output 6: int32 [8, 2048], P('dp')
All inputs are finite; a program needn't handle non-finite values.
Results may differ from a plain program's by a relative error of at most 0.02.
Values are sent between devices in bfloat16 or wider.
A program may use at most 1 GiB of HBM per device.

v0:
```python
import jax
import jax.numpy as jnp
from jax import lax
from jax.sharding import PartitionSpec as P

WINDOW = 2048
HEAD_DIM = 256
ROPE_DIM = 128
CONV_WIDTH = 4
SCORE_SCALE = 0.0625
NEG_BIG = -1e30


def rms_norm(hidden, norm_gain):
    hidden_f32 = hidden.astype(jnp.float32)
    inv_rms = lax.rsqrt(jnp.mean(hidden_f32 * hidden_f32, axis=-1, keepdims=True) + 1e-6)
    return (hidden_f32 * inv_rms * (1.0 + norm_gain.astype(jnp.float32))).astype(jnp.bfloat16)


def residual_add(hidden, update, bias_row):
    return (hidden.astype(jnp.float32) + update.astype(jnp.float32) + bias_row.astype(jnp.float32)).astype(jnp.bfloat16)


def linear_map(act_in, weight):
    return jnp.einsum('bcd,df->bcf', act_in, weight, preferred_element_type=jnp.float32)


def apply_rope(proj_f32, pos_exp):
    half_dim = ROPE_DIM // 2
    timescale = 10000.0 ** (2.0 * jnp.arange(half_dim).astype(jnp.float32) / ROPE_DIM)
    angle_rad = pos_exp.astype(jnp.float32) / timescale
    sin_a = jnp.sin(angle_rad)
    cos_a = jnp.cos(angle_rad)
    first_half = proj_f32[..., :half_dim]
    second_half = proj_f32[..., half_dim:ROPE_DIM]
    return jnp.concatenate([first_half * cos_a - second_half * sin_a, second_half * cos_a + first_half * sin_a, proj_f32[..., ROPE_DIM:]], axis=-1).astype(jnp.bfloat16)


def lru_combine(lhs_pair, rhs_pair):
    return lhs_pair[0] * rhs_pair[0], rhs_pair[0] * lhs_pair[1] + rhs_pair[1]


def recurrent_local(normed, is_reset, conv_prev, state_prev, w_x, b_x, w_y, b_y, conv_w, conv_b, w_a, b_a, w_i, b_i, a_param, w_out):
    tok_count = normed.shape[1]
    gate_y = jax.nn.gelu(linear_map(normed, w_y) + b_y.astype(jnp.float32), approximate=True).astype(jnp.bfloat16)
    branch_x = (linear_map(normed, w_x) + b_x.astype(jnp.float32)).astype(jnp.bfloat16)
    padded = jnp.concatenate([conv_prev, branch_x], axis=1)
    conv_f32 = conv_b.astype(jnp.float32) + sum(padded[:, tap_idx:tap_idx + tok_count].astype(jnp.float32) * conv_w[tap_idx].astype(jnp.float32) for tap_idx in range(CONV_WIDTH))
    conv_bf = conv_f32.astype(jnp.bfloat16)
    blocks = conv_bf.reshape(conv_bf.shape[:2] + w_a.shape[:2])
    gate_r = jax.nn.sigmoid(jnp.einsum('bchi,hij->bchj', blocks, w_a, preferred_element_type=jnp.float32).reshape(conv_bf.shape) + b_a.astype(jnp.float32))
    gate_i = jax.nn.sigmoid(jnp.einsum('bchi,hij->bchj', blocks, w_i, preferred_element_type=jnp.float32).reshape(conv_bf.shape) + b_i.astype(jnp.float32))
    decay_a = jnp.exp(-8.0 * gate_r * jax.nn.softplus(a_param))
    multiplier = jnp.where(is_reset, 1.0, jnp.sqrt(1.0 - decay_a * decay_a))
    decay_a = jnp.where(is_reset, 0.0, decay_a)
    is_first = (jnp.arange(tok_count) == 0)[None, :, None]
    drive_in = conv_bf.astype(jnp.float32) * gate_i * multiplier + jnp.where(is_first, decay_a * state_prev[:, None, :], 0.0)
    hidden_seq = lax.associative_scan(lru_combine, (decay_a, drive_in), axis=1)[1]
    mixed_hy = (hidden_seq * gate_y.astype(jnp.float32)).astype(jnp.bfloat16)
    return linear_map(mixed_hy, w_out), branch_x[:, tok_count - (CONV_WIDTH - 1):], hidden_seq[:, tok_count - 1]


def mlp_local(normed, w_1, b_1, w_2, b_2, w_d):
    gate_val = jax.nn.gelu(linear_map(normed, w_1) + b_1.astype(jnp.float32), approximate=True)
    up_val = linear_map(normed, w_2) + b_2.astype(jnp.float32)
    return linear_map((gate_val * up_val).astype(jnp.bfloat16), w_d)


def attention_local(normed, seg_pos, k_cache, v_cache, slot_pos, w_q, w_k, w_v, w_o):
    batch_size, tok_count = seg_pos.shape
    query_rot = apply_rope(linear_map(normed, w_q).reshape(batch_size, tok_count, -1, HEAD_DIM), seg_pos[:, :, None, None])
    key_new = apply_rope(linear_map(normed, w_k), seg_pos[:, :, None])
    value_new = linear_map(normed, w_v).astype(jnp.bfloat16)
    doc_id = jnp.cumsum((seg_pos == 0).astype(jnp.int32), axis=1)
    diff_old = seg_pos[:, :, None] - slot_pos[:, None, :]
    mask_old = (slot_pos[:, None, :] >= 0) & (diff_old >= 0) & (diff_old < WINDOW) & (doc_id[:, :, None] == 0)
    diff_new = seg_pos[:, :, None] - seg_pos[:, None, :]
    mask_new = (diff_new >= 0) & (diff_new < WINDOW) & (doc_id[:, :, None] == doc_id[:, None, :])
    score_old = jnp.where(mask_old[:, None], jnp.einsum('bchd,bwd->bhcw', query_rot, k_cache, preferred_element_type=jnp.float32) * SCORE_SCALE, NEG_BIG)
    score_new = jnp.where(mask_new[:, None], jnp.einsum('cdie,cle->cidl', query_rot, key_new, preferred_element_type=jnp.float32) * SCORE_SCALE, NEG_BIG)
    row_max = jnp.maximum(score_old.max(axis=-1), score_new.max(axis=-1))[..., None]
    exp_old = jnp.exp(score_old - row_max)
    exp_new = jnp.exp(score_new - row_max)
    denom_sum = exp_old.sum(axis=-1, keepdims=True) + exp_new.sum(axis=-1, keepdims=True)
    attn_out = jnp.einsum('bhcw,bwd->bchd', (exp_old / denom_sum).astype(jnp.bfloat16), v_cache, preferred_element_type=jnp.float32) + jnp.einsum('cidl,cle->cdie', (exp_new / denom_sum).astype(jnp.bfloat16), value_new, preferred_element_type=jnp.float32)
    attn_proj = linear_map(attn_out.astype(jnp.bfloat16).reshape(batch_size, tok_count, -1), w_o)
    batch_idx = jnp.arange(batch_size)[:, None]
    slot_new = jnp.mod(seg_pos, WINDOW)
    k_out = k_cache.at[batch_idx, slot_new].set(key_new, unique_indices=True)
    v_out = v_cache.at[batch_idx, slot_new].set(value_new, unique_indices=True)
    slot_out = slot_pos.at[batch_idx, slot_new].set(seg_pos, unique_indices=True)
    return attn_proj, k_out, v_out, slot_out


def gather_tokens(normed_loc):
    return lax.all_gather(normed_loc, 'tp', axis=1, tiled=True)


def scatter_sum(part_f32):
    return lax.psum_scatter(part_f32.astype(jnp.bfloat16), 'tp', scatter_dimension=1, tiled=True)


def solution(mesh):
    def device_body(x_in, seg_pos, conv_state, lru_state, k_cache, v_cache, slot_pos, norm_scale, w_x, b_x, w_y, b_y, conv_w, conv_b, w_a, b_a, w_i, b_i, a_param, w_out, b_out, w_q, w_k, w_v, w_o, b_o, w_1, b_1, w_2, b_2, w_d, b_d):
        is_reset = (seg_pos == 0)[:, :, None]
        hidden = x_in
        conv_list = []
        lru_list = []
        for layer_idx in range(2):
            normed = gather_tokens(rms_norm(hidden, norm_scale[2 * layer_idx]))
            rec_part, conv_new, lru_new = recurrent_local(normed, is_reset, conv_state[layer_idx], lru_state[layer_idx], w_x[layer_idx], b_x[layer_idx], w_y[layer_idx], b_y[layer_idx], conv_w[layer_idx], conv_b[layer_idx], w_a[layer_idx], b_a[layer_idx], w_i[layer_idx], b_i[layer_idx], a_param[layer_idx], w_out[layer_idx])
            hidden = residual_add(hidden, scatter_sum(rec_part), b_out[layer_idx])
            normed = gather_tokens(rms_norm(hidden, norm_scale[2 * layer_idx + 1]))
            mlp_part = mlp_local(normed, w_1[layer_idx], b_1[layer_idx], w_2[layer_idx], b_2[layer_idx], w_d[layer_idx])
            hidden = residual_add(hidden, scatter_sum(mlp_part), b_d[layer_idx])
            conv_list.append(conv_new)
            lru_list.append(lru_new)
        normed = gather_tokens(rms_norm(hidden, norm_scale[4]))
        attn_part, k_out, v_out, slot_out = attention_local(normed, seg_pos, k_cache, v_cache, slot_pos, w_q, w_k, w_v, w_o)
        hidden = residual_add(hidden, scatter_sum(attn_part), b_o)
        normed = gather_tokens(rms_norm(hidden, norm_scale[5]))
        mlp_part = mlp_local(normed, w_1[2], b_1[2], w_2[2], b_2[2], w_d[2])
        hidden = residual_add(hidden, scatter_sum(mlp_part), b_d[2])
        return hidden, jnp.stack(conv_list), jnp.stack(lru_list), k_out, v_out, slot_out

    col_spec = P(None, None, 'tp')
    vec_spec = P(None, 'tp')
    block_spec = P(None, 'tp', None, None)
    row_spec = P(None, 'tp', None)
    cache_spec = P('dp', None, None)
    arg_specs = (P('dp', 'tp', None), P('dp', None), P(None, 'dp', None, 'tp'), P(None, 'dp', 'tp'), cache_spec, cache_spec, P('dp', None), P(), col_spec, vec_spec, col_spec, vec_spec, col_spec, vec_spec, block_spec, vec_spec, block_spec, vec_spec, vec_spec, row_spec, P(), P(None, 'tp'), P(), P(), P('tp', None), P(), col_spec, vec_spec, col_spec, vec_spec, row_spec, P())
    result_specs = (P('dp', 'tp', None), P(None, 'dp', None, 'tp'), P(None, 'dp', 'tp'), cache_spec, cache_spec, P('dp', None))
    return jax.shard_map(device_body, mesh=mesh, in_specs=arg_specs, out_specs=result_specs, check_vma=False)
```

profile of v0, /device:TPU:0, one launch (start us, length us, event | category | flops | bytes accessed | tf_op | source)
XLA Modules:
  0.0 910.6 jit_solution(9736814926930018229)
XLA Ops:
  8.8 7.3 copy.195
  16.3 7.4 copy.196
  31.1 28.2 %all-gather.7.cloned.1.call-done = bf16[8,64,4096]{2,1,0:T(8,128)(2,1)} async-done(((bf16[8,8,4096]{2,1,0:T(8,128)(2,1)}), bf16[8,64,4096]{2,1,0:T(8,128)(2,1)}) %all-gather.7.cloned.1.call-update) | async-done | bytes 4194320 | tf_op jit(solution)/shard_map/all_gather | solution.py:96
  113.0 12.1 %fusion.361 = bf16[8,8,8,4096]{3,1,0,2:T(8,128)(2,1)} fusion(bf16[2,512,4096]{2,1,0:T(8,128)(2,1)} %param.51, bf16[8,64,4096]{2,1,0:T(8,128)(2,1)} %all-gather.7.cloned.1.call-done, bf16[2,4096,512]{2,1,0:T(8,128)(2,1)} %param.42, f32[8,64,512]{2,1,0:T(8,128)} %pad.84, f32[8,64,512]{2,1,0:T(8,128)S(1)} %pad.85, f32[512]{0:T(512)S(1)} %bitcast.539), kind=kOutput, calls=%fused_computation.445 | convolution fusion | flops 4300734464 | bytes 18876416 | tf_op jit(solution)/shard_map/bcd,df->bcf/dot_general | solution.py:25
  131.2 41.3 %reduce-scatter.19.cloned.1.call-done = bf16[8,32768]{1,0:T(8,128)(2,1)} async-done(((bf16[64,32768]{1,0:T(8,128)(2,1)}), bf16[8,32768]{1,0:T(8,128)(2,1)}) %reduce-scatter.19.cloned.1.call-update) | async-done | bytes 524304
  177.0 29.5 %all-gather.9.cloned.1.call-done = bf16[8,64,4096]{2,1,0:T(8,128)(2,1)} async-done(((bf16[8,8,4096]{2,1,0:T(8,128)(2,1)}), bf16[8,64,4096]{2,1,0:T(8,128)(2,1)}) %all-gather.9.cloned.1.call-update) | async-done | bytes 4194320 | tf_op jit(solution)/shard_map/all_gather | solution.py:96
  206.5 12.5 %fusion.102 = f32[8,64,1536]{2,1,0:T(8,128)} fusion(bf16[8,64,4096]{2,1,0:T(8,128)(2,1)} %all-gather.9.cloned.1.call-done, bf16[3,4096,1536]{2,1,0:T(8,128)(2,1)} %param.58, f32[1536]{0:T(1024)S(1)} %get-tuple-element.28), kind=kOutput, calls=%fused_computation.93 | convolution fusion | flops 6449528832 | bytes 19929088 | tf_op jit(solution)/shard_map/bcd,df->bcf/dot_general | solution.py:25
  219.0 21.5 %fusion.356 = bf16[8,8,8,4096]{3,1,0,2:T(8,128)(2,1)} fusion(bf16[3,1536,4096]{2,1,0:T(8,128)(2,1)} %param.62, f32[8,64,1536]{2,1,0:T(8,128)} %fusion.102, bf16[8,64,4096]{2,1,0:T(8,128)(2,1)} %all-gather.9.cloned.1.call-done, bf16[3,4096,1536]{2,1,0:T(8,128)(2,1)} %param.60, f32[1536]{0:T(1024)S(1)} %get-tuple-element.25), kind=kOutput, calls=%fused_computation.444 | convolution fusion | flops 12889358336 | bytes 36706304 | tf_op jit(solution)/shard_map/bcd,df->bcf/dot_general | solution.py:25
  246.6 41.3 %reduce-scatter.21.cloned.1.call-done = bf16[8,32768]{1,0:T(8,128)(2,1)} async-done(((bf16[64,32768]{1,0:T(8,128)(2,1)}), bf16[8,32768]{1,0:T(8,128)(2,1)}) %reduce-scatter.21.cloned.1.call-update) | async-done | bytes 524304
  292.3 30.4 %all-gather.11.cloned.1.call-done = bf16[8,64,4096]{2,1,0:T(8,128)(2,1)} async-done(((bf16[8,8,4096]{2,1,0:T(8,128)(2,1)}), bf16[8,64,4096]{2,1,0:T(8,128)(2,1)}) %all-gather.11.cloned.1.call-update) | async-done | bytes 4194320 | tf_op jit(solution)/shard_map/all_gather | solution.py:96
  376.4 12.1 %fusion.366 = bf16[8,8,8,4096]{3,1,0,2:T(8,128)(2,1)} fusion(bf16[2,512,4096]{2,1,0:T(8,128)(2,1)} %param.51, bf16[8,64,4096]{2,1,0:T(8,128)(2,1)} %all-gather.11.cloned.1.call-done, bf16[2,4096,512]{2,1,0:T(8,128)(2,1)} %param.42, f32[8,64,512]{2,1,0:T(8,128)} %pad.96, f32[8,64,512]{2,1,0:T(8,128)S(1)} %pad.97, f32[512]{0:T(512)S(1)} %bitcast.537), kind=kOutput, calls=%fused_computation.446 | convolution fusion | flops 4300734464 | bytes 18876416 | tf_op jit(solution)/shard_map/bcd,df->bcf/dot_general | solution.py:25
  393.5 42.4 %reduce-scatter.23.cloned.1.call-done = bf16[8,32768]{1,0:T(8,128)(2,1)} async-done(((bf16[64,32768]{1,0:T(8,128)(2,1)}), bf16[8,32768]{1,0:T(8,128)(2,1)}) %reduce-scatter.23.cloned.1.call-update) | async-done | bytes 524304
  439.0 30.8 %all-gather.13.cloned.1.call-done = bf16[8,64,4096]{2,1,0:T(8,128)(2,1)} async-done(((bf16[8,8,4096]{2,1,0:T(8,128)(2,1)}), bf16[8,64,4096]{2,1,0:T(8,128)(2,1)}) %all-gather.13.cloned.1.call-update) | async-done | bytes 4194320 | tf_op jit(solution)/shard_map/all_gather | solution.py:96
  469.9 12.5 %fusion.111 = f32[8,64,1536]{2,1,0:T(8,128)} fusion(bf16[8,64,4096]{2,1,0:T(8,128)(2,1)} %all-gather.13.cloned.1.call-done, bf16[3,4096,1536]{2,1,0:T(8,128)(2,1)} %param.58, f32[1536]{0:T(1024)S(1)} %copy-done.56), kind=kOutput, calls=%fused_computation.100 | convolution fusion | flops 6449528832 | bytes 19929088 | tf_op jit(solution)/shard_map/bcd,df->bcf/dot_general | solution.py:25
  482.4 21.5 %fusion.351 = bf16[8,8,8,4096]{3,1,0,2:T(8,128)(2,1)} fusion(bf16[3,1536,4096]{2,1,0:T(8,128)(2,1)} %param.62, f32[8,64,1536]{2,1,0:T(8,128)} %fusion.111, bf16[8,64,4096]{2,1,0:T(8,128)(2,1)} %all-gather.13.cloned.1.call-done, bf16[3,4096,1536]{2,1,0:T(8,128)(2,1)} %param.60, f32[1536]{0:T(1024)S(1)} %copy-done.57), kind=kOutput, calls=%fused_computation.443 | convolution fusion | flops 12889358336 | bytes 36706304 | tf_op jit(solution)/shard_map/bcd,df->bcf/dot_general | solution.py:25
  508.7 42.5 %reduce-scatter.25.cloned.1.call-done = bf16[8,32768]{1,0:T(8,128)(2,1)} async-done(((bf16[64,32768]{1,0:T(8,128)(2,1)}), bf16[8,32768]{1,0:T(8,128)(2,1)}) %reduce-scatter.25.cloned.1.call-update) | async-done | bytes 524304
  557.7 28.4 %all-gather.15.cloned.1.call-done = bf16[8,64,4096]{2,1,0:T(8,128)(2,1)} async-done(((bf16[8,8,4096]{2,1,0:T(8,128)(2,1)}), bf16[8,64,4096]{2,1,0:T(8,128)(2,1)}) %all-gather.15.cloned.1.call-update) | async-done | bytes 4194320 | tf_op jit(solution)/shard_map/all_gather | solution.py:96
  631.9 41.9 %reduce-scatter.27.cloned.1.call-done = bf16[8,32768]{1,0:T(8,128)(2,1)} async-done(((bf16[64,32768]{1,0:T(8,128)(2,1)}), bf16[8,32768]{1,0:T(8,128)(2,1)}) %reduce-scatter.27.cloned.1.call-update) | async-done | bytes 524304
  677.0 30.8 %all-gather.17.cloned.1.call-done = bf16[8,64,4096]{2,1,0:T(8,128)(2,1)} async-done(((bf16[8,8,4096]{2,1,0:T(8,128)(2,1)}), bf16[8,64,4096]{2,1,0:T(8,128)(2,1)}) %all-gather.17.cloned.1.call-update) | async-done | bytes 4194320 | tf_op jit(solution)/shard_map/all_gather | solution.py:96
  707.9 12.5 %fusion.120 = f32[8,64,1536]{2,1,0:T(8,128)} fusion(bf16[8,64,4096]{2,1,0:T(8,128)(2,1)} %all-gather.17.cloned.1.call-done, bf16[3,4096,1536]{2,1,0:T(8,128)(2,1)} %param.58, f32[1536]{0:T(1024)S(1)} %copy-done.54), kind=kOutput, calls=%fused_computation.107 | convolution fusion | flops 6449528832 | bytes 19929088 | tf_op jit(solution)/shard_map/bcd,df->bcf/dot_general | solution.py:25
  720.4 21.5 %fusion.346 = bf16[8,8,8,4096]{3,1,0,2:T(8,128)(2,1)} fusion(bf16[3,1536,4096]{2,1,0:T(8,128)(2,1)} %param.62, f32[8,64,1536]{2,1,0:T(8,128)} %fusion.120, bf16[8,64,4096]{2,1,0:T(8,128)(2,1)} %all-gather.17.cloned.1.call-done, bf16[3,4096,1536]{2,1,0:T(8,128)(2,1)} %param.60, f32[1536]{0:T(1024)S(1)} %copy-done.55), kind=kOutput, calls=%fused_computation.442 | convolution fusion | flops 12889358336 | bytes 36706304 | tf_op jit(solution)/shard_map/bcd,df->bcf/dot_general | solution.py:25
  746.8 24.1 %scatter_fusion.2 = s32[8,2048]{1,0:T(8,128)S(1)} fusion(s32[8,2048]{1,0:T(8,128)S(1)} %copy-done.1, s32[512]{0:T(512)S(1)} %reshape.450, s32[512]{0:T(512)S(1)} %reshape.464), kind=kCustom, calls=%fused_computation.2 | custom fusion | bytes 10240 | tf_op jit(solution)/shard_map/scatter | solution.py:91
  775.2 62.6 %scatter_fusion = bf16[8,2048,256]{2,1,0:T(8,128)(2,1)} fusion(bf16[8,2048,256]{2,1,0:T(8,128)(2,1)} %copy.195, s32[512]{0:T(512)S(1)} %reshape.450, bf16[512,256]{1,0:T(8,128)(2,1)S(1)} %bitcast.471), kind=kCustom, calls=%fused_computation | custom fusion | bytes 790528 | tf_op jit(solution)/shard_map/scatter | solution.py:89
  837.8 63.0 %scatter_fusion.1 = bf16[8,2048,256]{2,1,0:T(8,128)(2,1)} fusion(bf16[8,2048,256]{2,1,0:T(8,128)(2,1)} %copy.196, s32[512]{0:T(512)S(1)} %reshape.450, bf16[512,256]{1,0:T(8,128)(2,1)S(1)} %bitcast.491), kind=kCustom, calls=%fused_computation.1 | custom fusion | bytes 790528 | tf_op jit(solution)/shard_map/scatter | solution.py:90
  (393 shorter events, 216.0 us)
Async XLA Ops:
  7.2 591.8 %copy-start = (bf16[4096,256]{1,0:T(8,128)(2,1)S(1)}, bf16[4096,256]{1,0:T(8,128)(2,1)}, u32[]{:S(2)}) copy-start(bf16[4096,256]{1,0:T(8,128)(2,1)} %param.54) | copy-start | bytes 6291460
  7.2 52.1 %all-gather.7.cloned.1.call-start = ((), (), s32[]{:S(2)}) async-start(), calls=%async_computation.6 | async-start | bytes 4718592 | tf_op jit(solution)/shard_map/all_gather | solution.py:96
  25.6 146.9 %reduce-scatter.19.cloned.1.call-start = ((), (), s32[]{:S(2)}) async-start(), calls=%async_computation.12 | async-start | bytes 4718592
  129.9 45.8 %copy-start.39 = (bf16[3,1536]{1,0:T(4,128)(2,1)S(1)}, bf16[3,1536]{1,0:T(4,128)(2,1)}, u32[]{:S(2)}) copy-start(bf16[3,1536]{1,0:T(4,128)(2,1)} %param.59) | copy-start | bytes 27652
  129.9 46.5 %copy-start.40 = (bf16[3,1536]{1,0:T(4,128)(2,1)S(1)}, bf16[3,1536]{1,0:T(4,128)(2,1)}, u32[]{:S(2)}) copy-start(bf16[3,1536]{1,0:T(4,128)(2,1)} %param.61) | copy-start | bytes 27652
  129.9 76.6 %all-gather.9.cloned.1.call-start = ((), (), s32[]{:S(2)}) async-start(), calls=%async_computation.7 | async-start | bytes 4718592 | tf_op jit(solution)/shard_map/all_gather | solution.py:96
  175.6 112.3 %reduce-scatter.21.cloned.1.call-start = ((), (), s32[]{:S(2)}) async-start(), calls=%async_computation.13 | async-start | bytes 4718592
  245.2 47.0 %copy-start.22 = (bf16[1,8,3,512]{3,1,2,0:T(8,128)(2,1)S(1)}, bf16[1,8,3,512]{3,1,2,0:T(8,128)(2,1)}, u32[]{:S(2)}) copy-start(bf16[1,8,3,512]{3,1,2,0:T(8,128)(2,1)} %get-tuple-element.78) | copy-start | bytes 73732
  245.2 47.1 %copy-start.53 = (f32[1,512]{1,0:T(1,128)S(1)}, f32[1,512]{1,0:T(1,128)}, u32[]{:S(2)}) copy-start(f32[1,512]{1,0:T(1,128)} %get-tuple-element.101) | copy-start | bytes 6148
  245.2 77.5 %copy-start.62 = (f32[1,512]{1,0:T(1,128)S(1)}, f32[1,512]{1,0:T(1,128)}, u32[]{:S(2)}) copy-start(f32[1,512]{1,0:T(1,128)} %get-tuple-element.111) | copy-start | bytes 6148
  245.3 77.4 %all-gather.11.cloned.1.call-start = ((), (), s32[]{:S(2)}) async-start(), calls=%async_computation.8 | async-start | bytes 4718592 | tf_op jit(solution)/shard_map/all_gather | solution.py:96
  291.8 144.1 %reduce-scatter.23.cloned.1.call-start = ((), (), s32[]{:S(2)}) async-start(), calls=%async_computation.14 | async-start | bytes 4718592
  393.2 76.7 %copy-start.56 = (f32[1536]{0:T(1024)S(1)}, f32[1536]{0:T(1024)}, u32[]{:S(2)}) copy-start(f32[1536]{0:T(1024)} %get-tuple-element.29) | copy-start | bytes 18436
  393.2 76.6 %all-gather.13.cloned.1.call-start = ((), (), s32[]{:S(2)}) async-start(), calls=%async_computation.9 | async-start | bytes 4718592 | tf_op jit(solution)/shard_map/all_gather | solution.py:96
  439.0 112.3 %reduce-scatter.25.cloned.1.call-start = ((), (), s32[]{:S(2)}) async-start(), calls=%async_computation.15 | async-start | bytes 4718592
  508.6 47.2 %copy-start.1 = (s32[8,2048]{1,0:T(8,128)S(1)}, s32[8,2048]{1,0:T(8,128)}, u32[]{:S(2)}) copy-start(s32[8,2048]{1,0:T(8,128)} %copy.197) | copy-start | bytes 196612
  508.7 77.4 %all-gather.15.cloned.1.call-start = ((), (), s32[]{:S(2)}) async-start(), calls=%async_computation.10 | async-start | bytes 4718592 | tf_op jit(solution)/shard_map/all_gather | solution.py:96
  555.2 118.7 %reduce-scatter.27.cloned.1.call-start = ((), (), s32[]{:S(2)}) async-start(), calls=%async_computation.16 | async-start | bytes 4718592
  631.2 76.6 %copy-start.54 = (f32[1536]{0:T(1024)S(1)}, f32[1536]{0:T(1024)}, u32[]{:S(2)}) copy-start(f32[1536]{0:T(1024)} %get-tuple-element.27) | copy-start | bytes 18436
  631.2 76.6 %all-gather.17.cloned.1.call-start = ((), (), s32[]{:S(2)}) async-start(), calls=%async_computation.11 | async-start | bytes 4718592 | tf_op jit(solution)/shard_map/all_gather | solution.py:96
  677.0 223.9 %reduce-scatter.29.cloned.1.call-start = ((), (), s32[]{:S(2)}) async-start(), calls=%async_computation.17 | async-start | bytes 4718592
  770.9 129.9 %copy-start.2 = (s32[8,2048]{1,0:T(8,128)}, s32[8,2048]{1,0:T(8,128)S(1)}, u32[]{:S(2)}) copy-start(s32[8,2048]{1,0:T(8,128)S(1)} %scatter_fusion.2) | copy-start | bytes 196612
  770.9 66.9 %copy-start.19 = (bf16[8,64,256]{2,1,0:T(8,128)(2,1)S(1)}, bf16[8,64,256]{2,1,0:T(8,128)(2,1)}, u32[]{:S(2)}) copy-start(bf16[8,64,256]{2,1,0:T(8,128)(2,1)} %copy-done.18) | copy-start | bytes 786436
  775.2 126.9 %copy-start.31 = (f32[1,4096]{1,0:T(1,128)S(1)}, f32[1,4096]{1,0:T(1,128)}, u32[]{:S(2)}) copy-start(f32[1,4096]{1,0:T(1,128)} %get-tuple-element.80) | copy-start | bytes 49156
  (56 other events, 792.0 us)
Sparse Core Ops, SparseCore 0:
  25.7 33.5 all-gather.6
  130.0 42.4 reduce-scatter.18
  175.7 30.7 all-gather.8
  245.4 42.4 reduce-scatter.20
  291.9 30.7 all-gather.10
  393.4 42.4 reduce-scatter.22
  439.1 30.7 all-gather.12
  508.8 42.4 reduce-scatter.24
  555.3 30.7 all-gather.14
  631.4 42.4 reduce-scatter.26
  677.1 30.7 all-gather.16
  746.7 42.4 reduce-scatter.28
where the time goes:
time: 925 us; the launch traced here: 911 us
  waiting for transfers between devices  388 us (42%)
  local copies, waits for them, and re-layouts  283 us (31%)
  matrix products  168 us (18%)
  other arithmetic  53.6 us (6%)
  between operations  16.1 us (2%)
    unnamed x18, waiting for transfers between devices  210 us
    all_gather x6, waiting for transfers between devices, gather_tokens(): return lax.all_gather(normed_loc, 'tp', axis=1, tiled=True)  178 us
    dot_general x14, matrix products, linear_map(): jnp.einsum('bcd,df->bcf', act_in, weight, preferred_element_type=jnp.floa...  154 us
    scatter x1, local copies, waits for them, and re-layouts, attention_local(): v_out = v_cache.at[batch_idx, slot_new].set(value_new, unique_indices=True)  63 us
    scatter x1, local copies, waits for them, and re-layouts, attention_local(): k_out = k_cache.at[batch_idx, slot_new].set(key_new, unique_indices=True)  62.6 us
    unnamed x157, local copies, waits for them, and re-layouts  55.4 us
    slice x64, local copies, waits for them, and re-layouts, recurrent_local(): lax.associative_scan(lru_combine, (decay_a, drive_in), axis=1)[1]  45.6 us
    scatter x1, local copies, waits for them, and re-layouts, attention_local(): slot_pos.at[batch_idx, slot_new].set(seg_pos, unique_indices=True)  24.1 us
  transfers between devices with their start and end apart: 12, of which 11 were waited for; matrix products, arithmetic and copies ran while one was open for 18% of the time, Pallas kernels for 0%

commit v1 on v0

v1 whole, which is shorter than its diff:
```python
import jax
import jax.numpy as jnp
from jax import lax
from jax.experimental import pallas as pl
from jax.experimental.pallas import tpu as pltpu
from jax.sharding import PartitionSpec as P

F32 = jnp.float32
BF16 = jnp.bfloat16
WINDOW = 2048
ROPE_DIM = 128
D = 4096
HALF_SEQ = 4
TOK = 8
SHARD = 32
ROWS = 256
COLS = 512
NBLK = D // COLS
PIECE = 16
NC = 4
NR = 4
WID = 256
HALVES = LAYERS = 2
SEQS = 8
SPAN = 96
NEG = -1e30

REC, MLP, ATT = 'rec', 'mlp', 'att'
SUBLAYERS = ((REC, 0), (MLP, 0), (REC, 1), (MLP, 1), (ATT, 0), (MLP, 2))

AG_OWN = ('x0', 'y1', 'x1', 'y0', 'so')
AG_STEPS = (
    (('x0', 'y1'), ('dy0', 'dx1', 'sx0', 'sy1')),
    (('x1', 'y0'), ('sx1', 'sy0')),
    (('dy0', 'dx1'), ('sd0', 'sd1')),
    (('so', 'sx0', 'sy1', 'sx1', 'sy0', 'sd0', 'sd1'), ()),
)
AG_STEP_OF = {name: i for i, (waits, _) in enumerate(AG_STEPS) for name in waits}
AG_ROWS = tuple(sum(SHARD if name == 'so' else PIECE for name in waits) for waits, _ in AG_STEPS)
RS_IN = ('x0', 'y1', 'x1', 'y0')
CHUNKS = 2
CBLK = NBLK // CHUNKS
RS_SEMS = 3 * CHUNKS + 1
RS_ORDER = ((0, 0), (1, 0), (0, 1), (1, 1), (2, 0), (2, 1))

UNITS = {REC: (2, 2.4, 2, 0.6), MLP: (6, 1.4, 8, 0.6), ATT: (6, 1.7, 2, 0.6)}
LINK_US, D2D_US, LINK_LATENCY, D2D_LATENCY = 2.81, 0.22, 1.9, 1.0


def link_of(name):
    if name[0] == 's':
        return 's'
    return 'x' if name in ('x0', 'x1', 'dx1', 'd0') else 'y'


def plan():
    free = dict.fromkeys('xys', 0.0)
    ends = {}
    now = 0.0

    def send(key, size):
        link = link_of(key[-1])
        rate, latency = (D2D_US, D2D_LATENCY) if link == 's' else (LINK_US, LINK_LATENCY)
        free[link] = max(now, free[link]) + size * rate
        ends[key] = free[link] + latency

    def own(h, k):
        for name in AG_OWN:
            send((h, k, 'g', name), 2 if name == 'so' else 1)

    def chain(h):
        steps = []
        for k, (kind, _) in enumerate(SUBLAYERS):
            n_col, _, n_row, _ = UNITS[kind]
            for i, (waits, sends) in enumerate(AG_STEPS):
                steps.append((('ag', i, 0, h, k), 0, [(h, k, 'g', w) for w in waits], [((h, k, 'g', w), 1) for w in sends], 0))
            for step, c in RS_ORDER:
                need = n_col + n_row * (c + 1) // CHUNKS if step == 0 else 0
                waits = ((), ('s3', 's1', 's2', 's0'), ('d0', 'd1'))[step]
                sends = (('s3', 's1', 's2', 's0'), ('d0', 'd1', 'x0', 'y1'), ('y0', 'x1'))[step]
                steps.append((('rs', step, c, h, k), need, [(h, k, c, w) for w in waits],
                              [((h, k, c, w), (2 if step == 0 else 1) / CHUNKS) for w in sends], 0.15))
            steps.append((('rs', 3, 0, h, k), 0, [(h, k, c, w) for c in range(CHUNKS) for w in RS_IN], [], 0.7))
        return steps

    waiting = [chain(0), chain(1)]
    computing = [(h, k) for k in range(len(SUBLAYERS)) for h in range(2)]
    unit, done, gathered, order = 0, {}, set(), []
    own(0, 0)
    own(1, 0)
    while waiting[0] or waiting[1]:
        heads = []
        for h in range(2):
            if waiting[h]:
                step = waiting[h][0]
                if done.get((h, step[0][-1]), 0) >= step[1]:
                    heads.append((max([ends[w] for w in step[2]], default=0.0), step[0][-1], h))
        ready = [(k, h) for t, k, h in heads if t <= now]
        if not ready and computing and computing[0] in gathered:
            h, k = computing[0]
            n_col, col_us, n_row, row_us = UNITS[SUBLAYERS[k][0]]
            now += col_us if unit < n_col else row_us
            order.append(('unit', h, k))
            unit += 1
            done[h, k] = unit
            if unit == n_col + n_row:
                computing.pop(0)
                unit = 0
            continue
        if ready:
            h = min(ready)[1]
        else:
            now, _, h = min(heads)
        name, _, _, sends, us = waiting[h].pop(0)
        k = name[-1]
        now += us
        for key, size in sends:
            send(key, size)
        if name[:2] == ('ag', 3):
            gathered.add((h, k))
        if name[:2] == ('rs', 3) and k + 1 < len(SUBLAYERS):
            own(h, k + 1)
        order.append(name)
    return order


class Ring:
    def __init__(self, depth, order, start):
        self.depth, self.start, self.at = depth, start, 0
        self.total = sum(n for _, n in order)
        self.runs = []
        g = 0
        for what, n in order:
            self.runs.append((what, g, n))
            g += n

    def prime(self):
        for what, g0, n in self.runs:
            for t in range(n):
                if g0 + t < self.depth:
                    self.start(what, t, g0 + t)

    def take(self, n):
        base = self.at
        self.at += n
        return base

    def slot(self, base, i):
        return (base + i) % self.depth

    def refill(self, base, n, i):
        ahead = base + self.depth
        slot = self.slot(base, i)
        for what, g0, m in self.runs:
            lo, hi = max(g0, ahead), min(g0 + m, ahead + n)
            if lo < hi:
                if isinstance(i, int):
                    if lo - ahead <= i < hi - ahead:
                        self.start(what, ahead - g0 + i, slot)
                else:
                    @pl.when((i >= lo - ahead) & (i < hi - ahead))
                    def _():
                        self.start(what, ahead - g0 + i, slot)


def loop(n, body):
    def step(i, carry):
        body(i, None)
        return carry

    lax.fori_loop(0, n, step, 0)


def sum_blocks(body):
    return lax.fori_loop(0, NBLK, body, jnp.zeros((SHARD, COLS), F32))


def row_sum(v):
    return jnp.sum(v, axis=-1, keepdims=True)


def row_max(v):
    return jnp.max(v, axis=-1, keepdims=True)


def run_ticks(i, ticks):
    for when, fn in ticks.items():
        if isinstance(i, int):
            if i == when:
                fn()
        else:
            pl.when(i == when)(fn)


def later(ticks, n):
    return {i - n: fn for i, fn in ticks.items()}


def mega(x_ref, norm_ref, bout_ref, bo_ref, bd_ref, by_ref, bx_ref, cw_ref, cb_ref, ba_ref, bi_ref, ap_ref, b1_ref, b2_ref,
         conv_ref, lru_ref, wa_ref, wi_ref, pos_ref, slot_ref, cos_ref, sin_ref,
         w_y, w_x, w_out, w_1, w_2, w_d, w_q, w_k, w_v, w_o, k_cache, v_cache,
         xo_ref, convo_ref, lruo_ref, ko_ref, vo_ref,
         nbuf, part, sibr, town, tbuf, dgr, xyr, xres, hbuf, qbuf, obuf, kvbuf, cring, rring,
         gain, bias, rvec, mvec, conv0, convf, poscol, posrow,
         ag_s, ag_r, rs_s, rs_r, csem, rsem, kvsem):
    me = lax.axis_index('tp')
    core = lax.rem(me, 2)
    xpos = lax.rem(me // 2, 2)
    ypos = me // 4
    sib = me + 1 - 2 * core
    xn = me + 2 - 4 * xpos
    yn = me + 4 - 8 * ypos
    dg = xn + 4 - 8 * ypos

    def start_c(what, t, slot):
        kind, l = what
        cols = pl.ds(t * WID if isinstance(t, int) else pl.multiple_of(t * WID, WID), WID)
        if kind == REC:
            srcs = w_y.at[l, :, cols], w_x.at[l, :, cols]
        elif kind == MLP:
            srcs = w_1.at[l, :, cols], w_2.at[l, :, cols]
        elif kind == 'q':
            srcs = w_q.at[:, pl.ds(0, WID)], w_q.at[:, pl.ds(WID, WID)]
        else:
            srcs = w_k, w_v
        for e, src in enumerate(srcs):
            pltpu.make_async_copy(src, cring.at[slot, e], csem.at[slot, e]).start()

    def wait_c(slot):
        for e, src in enumerate((w_k, w_v)):
            pltpu.make_async_copy(src, cring.at[slot, e], csem.at[slot, e]).wait()

    def start_r(what, t, slot):
        kind, l = what
        if kind == MLP:
            cols = pl.ds(t * COLS if isinstance(t, int) else pl.multiple_of(t * COLS, COLS), COLS)
            for e in range(3):
                pltpu.make_async_copy(w_d.at[l, pl.ds(e * 512, 512), cols], rring.at[slot, e], rsem.at[slot, e]).start()
        else:
            for e in range(4):
                c0 = t * 4 * COLS + e * COLS
                cols = pl.ds(c0 if isinstance(t, int) else pl.multiple_of(c0, COLS), COLS)
                src = w_out.at[l, :, cols] if kind == REC else w_o.at[:, cols]
                pltpu.make_async_copy(src, rring.at[slot, e], rsem.at[slot, e]).start()

    def wait_r(slot, n):
        for e in range(n):
            pltpu.make_async_copy(w_o.at[:, pl.ds(0, COLS)], rring.at[slot, e], rsem.at[slot, e]).wait()

    c_order, r_order = [], []
    for kind, l in SUBLAYERS:
        for _ in range(2):
            if kind == REC:
                c_order.append(((REC, l), 2))
                r_order.append(((REC, l), 2))
            elif kind == MLP:
                c_order.append(((MLP, l), 6))
                r_order.append(((MLP, l), 8))
            else:
                c_order += [(('q', 0), 1), (('kv', 0), 1)]
                r_order.append(((ATT, 0), 2))
    cw = Ring(NC, c_order, start_c)
    rw = Ring(NR, r_order, start_r)

    def kv_copies(seq, slot):
        return (pltpu.make_async_copy(k_cache.at[seq], kvbuf.at[slot, 0], kvsem.at[slot, 0]),
                pltpu.make_async_copy(v_cache.at[seq], kvbuf.at[slot, 1], kvsem.at[slot, 1]))

    def await_bytes(ref, sem):
        pltpu.make_async_copy(ref, ref, sem).wait()

    def rows_of(dev, p=None):
        if p is None:
            return pl.ds(pl.multiple_of(SHARD * dev, SHARD), SHARD)
        return pl.ds(pl.multiple_of(SHARD * dev + PIECE * p, PIECE), PIECE)

    def ag(h, name):
        p = None if name == 'so' else int(name[-1])
        origin = {'so': me, 'x': me, 'y': me, 'dy': xn, 'dx': yn, 'sx': xn, 'sy': yn, 'sd': dg}[name if name == 'so' else name[:-1]]
        target = sib if name[0] == 's' else xn if name in ('x0', 'x1', 'dx1') else yn
        ref = nbuf.at[h, rows_of(origin, p), :]
        return pltpu.make_async_remote_copy(src_ref=ref, dst_ref=ref, send_sem=ag_s.at[h], recv_sem=ag_r.at[h, AG_STEP_OF[name]],
                                            device_id={'tp': target}, device_id_type=pl.DeviceIdType.MESH)

    def ag0(h):
        for name in AG_OWN:
            ag(h, name).start()

    def ag_step(h, i):
        waits, sends = AG_STEPS[i]
        await_bytes(nbuf.at[h, pl.ds(0, AG_ROWS[i]), :], ag_r.at[h, i])
        for name in sends:
            ag(h, name).start()
        if i == 3:
            await_bytes(nbuf.at[h, pl.ds(0, sum(AG_ROWS)), :], ag_s.at[h])

    chip_rows = (me, xn, yn, dg)
    other_rows = (sib, xn + 1 - 2 * core, yn + 1 - 2 * core, dg + 1 - 2 * core)

    def rs_sem(name, c):
        if name in RS_IN:
            return RS_SEMS - 1
        return c * 3 + (0 if name == 's3' else 1 if name[0] == 's' else 2)

    def rs(h, name, c):
        p = int(name[1])
        cb = pl.ds(c * CBLK, CBLK)
        if name[0] == 's':
            src, dst, target = part.at[h, cb, rows_of(other_rows[p]), :], sibr.at[h, p, cb], sib
        elif name[0] == 'd':
            src, dst, target = tbuf.at[h, 2, p, cb], dgr.at[h, p, cb], (xn if p == 0 else yn)
        elif name[0] == 'x':
            src, dst, target = tbuf.at[h, 0, p, cb], xyr.at[h, 0, p, cb], xn
        else:
            src, dst, target = tbuf.at[h, 1, p, cb], xyr.at[h, 1, p, cb], yn
        return pltpu.make_async_remote_copy(src_ref=src, dst_ref=dst, send_sem=rs_s.at[h], recv_sem=rs_r.at[h, rs_sem(name, c)],
                                            device_id={'tp': target}, device_id_type=pl.DeviceIdType.MESH)

    def rs0(h, c):
        for p in (3, 1, 2, 0):
            rs(h, 's%d' % p, c).start()

    def rs1(h, c):
        cb = pl.ds(c * CBLK, CBLK)

        def some(p):
            def body(i, _):
                j = c * CBLK + i
                v = part[h, j, rows_of(chip_rows[p]), :].astype(F32) + sibr[h, p, j].astype(F32)
                if p == 0:
                    town[h, j] = v
                else:
                    v = v.astype(BF16)
                    tbuf[h, p - 1, 0, j] = v[:PIECE]
                    tbuf[h, p - 1, 1, j] = v[PIECE:]

            loop(CBLK, body)

        await_bytes(sibr.at[h, 3, cb], rs_r.at[h, rs_sem('s3', c)])
        some(3)
        rs(h, 'd0', c).start()
        rs(h, 'd1', c).start()
        await_bytes(sibr.at[h, pl.ds(0, 3), cb], rs_r.at[h, rs_sem('s0', c)])
        some(1)
        rs(h, 'x0', c).start()
        some(2)
        rs(h, 'y1', c).start()
        some(0)

    def rs2(h, c):
        await_bytes(dgr.at[h, :, pl.ds(c * CBLK, CBLK)], rs_r.at[h, rs_sem('d0', c)])

        def body(i, _):
            j = c * CBLK + i
            for to, p in ((1, 0), (0, 1)):
                tbuf[h, to, p, j] = (tbuf[h, to, p, j].astype(F32) + dgr[h, p, j].astype(F32)).astype(BF16)

        loop(CBLK, body)
        rs(h, 'y0', c).start()
        rs(h, 'x1', c).start()

    def blk(j):
        return pl.ds(pl.multiple_of(j * COLS, COLS), COLS)

    def normalise(h, k, square_sum):
        inv = lax.rsqrt(row_sum(square_sum) * (1.0 / D) + 1e-6)

        def body(j, _):
            nbuf[h, rows_of(me), blk(j)] = (xres[h, j].astype(F32) * inv * gain[k:k + 1, blk(j)]).astype(BF16)

        loop(NBLK, body)

    def first(h):
        def body(j, acc):
            v = x_ref[h * SHARD:(h + 1) * SHARD, blk(j)]
            xres[h, j] = v
            v = v.astype(F32)
            return acc + v * v

        normalise(h, 0, sum_blocks(body))
        ag0(h)

    def rs3(h, k):
        await_bytes(xyr.at[h], rs_r.at[h, RS_SEMS - 1])
        last = k == len(SUBLAYERS) - 1

        def body(j, acc):
            got = jnp.concatenate([xyr[h, 0, p, j].astype(F32) + xyr[h, 1, p, j].astype(F32) for p in range(2)], axis=0)
            v = xres[h, j].astype(F32) + (town[h, j] + got) + bias[k:k + 1, blk(j)]
            v = v.astype(BF16)
            if last:
                xo_ref[h * SHARD:(h + 1) * SHARD, blk(j)] = v
                return acc
            xres[h, j] = v
            v = v.astype(F32)
            return acc + v * v

        square_sum = sum_blocks(body)
        await_bytes(part.at[h, :, pl.ds(0, ROWS - SHARD), :], rs_s.at[h])
        if not last:
            normalise(h, k + 1, square_sum)
            ag0(h)

    def setup():
        for k, (ref, l) in enumerate(((bout_ref, 0), (bd_ref, 0), (bout_ref, 1), (bd_ref, 1), (bo_ref, 0), (bd_ref, 2))):
            bias[k:k + 1, :] = ref[...].astype(F32)[l:l + 1]
        rows = [(by_ref[...], 1), (bx_ref[...], 1)] + [(cw_ref[:, i], 1) for i in range(4)]
        rows += [(cb_ref[...], 1), (ba_ref[...], 1), (bi_ref[...], 1), (jax.nn.softplus(ap_ref[...]), -8.0)]
        for r, (v, scale) in enumerate(rows):
            v = v.astype(F32) * scale
            for l in range(LAYERS):
                for t in range(2):
                    rvec[l, t, r:r + 1, :] = v[l:l + 1, t * WID:(t + 1) * WID]
        for r, ref in enumerate((b1_ref, b2_ref)):
            v = ref[...].astype(F32)
            for m in range(3):
                for t in range(6):
                    mvec[m, t, r:r + 1, :] = v[m:m + 1, t * WID:(t + 1) * WID]
        conv0[...] = jnp.zeros_like(conv0)
        for l in range(LAYERS):
            for i in range(3):
                v = conv_ref[l, i].astype(F32)
                for q in range(SEQS):
                    conv0[l, q, 5 + i:6 + i, :] = v[q:q + 1]
        p = pos_ref[...]
        cols = jnp.concatenate([p, p], axis=1).T
        for q in range(SEQS):
            col = cols[:, q:q + 1]
            poscol[q] = col
            posrow[q // HALF_SEQ, :, q % HALF_SEQ] = col[:64].reshape(8, TOK, 1)

    def dot(a, b):
        return jnp.dot(a, b, preferred_element_type=F32)

    def store_part(h, j, v):
        part[h, j] = v.astype(BF16)

    def out_small(h, ticks):
        base = rw.take(2)

        def body(i, _):
            slot = rw.slot(base, i)
            wait_r(slot, 4)
            for e in range(4):
                store_part(h, i * 4 + e, dot(hbuf[:, 0:512], rring[slot, e]))
            rw.refill(base, 2, i)
            run_ticks(i, ticks)

        loop(2, body)

    def comp_rec(h, l, ticks):
        base = cw.take(2)

        def body(t, _):
            slot = cw.slot(base, t)
            wait_c(slot)
            vec = rvec[l, t]
            lanes = pl.ds(pl.multiple_of(t * WID, WID), WID)

            def row(r):
                return vec[r:r + 1, :]

            n = nbuf[h]
            gate_y = jax.nn.gelu(dot(n, cring[slot, 0]) + row(0), approximate=True).astype(BF16).astype(F32)
            u = (dot(n, cring[slot, 1]) + row(1)).astype(BF16).astype(F32)
            cw.refill(base, 2, t)
            u3 = u.reshape(SHARD, TOK, WID)
            for q in range(HALF_SEQ):
                for i in range(3):
                    convf[l, i, h * HALF_SEQ + q:h * HALF_SEQ + q + 1, lanes] = u3[SHARD - HALF_SEQ + q, 5 + i:6 + i, :]
            before = jnp.concatenate([conv0[l, h * HALF_SEQ:(h + 1) * HALF_SEQ, :, lanes], u3[:SHARD - HALF_SEQ]], axis=0)
            jj = lax.broadcasted_iota(jnp.int32, (SHARD, TOK, WID), 1)
            conv = u3 * row(5)
            for back in (1, 2, 3):
                shifted = jnp.where(jj >= back, pltpu.roll(u3, back, 1), pltpu.roll(before, back, 1))
                conv = conv + shifted * row(5 - back)
            conv = (conv + row(6)).reshape(ROWS, WID).astype(BF16)
            gate_r = jax.nn.sigmoid(dot(conv, wa_ref[l, t]) + row(7))
            gate_i = jax.nn.sigmoid(dot(conv, wi_ref[l, t]) + row(8))
            decay = jnp.exp(gate_r * row(9))
            fresh = posrow[h].reshape(ROWS, 1) == 0
            mult = jnp.where(fresh, 1.0, jnp.sqrt(1.0 - decay * decay))
            decay = jnp.where(fresh, 0.0, decay)
            drive = conv.astype(F32) * gate_i * mult
            a3 = decay.reshape(SHARD, TOK, WID)
            b3 = drive.reshape(SHARD, TOK, WID)
            for back in (1, 2, 4):
                b3 = b3 + a3 * jnp.where(jj >= back, pltpu.roll(b3, back, 1), 0.0)
                a3 = a3 * jnp.where(jj >= back, pltpu.roll(a3, back, 1), 1.0)
            held = lru_ref[l, :, lanes]
            carry = jnp.concatenate([held[q:q + 1].reshape(1, 1, WID) for q in range(h * HALF_SEQ, (h + 1) * HALF_SEQ)], axis=0)
            out = []
            for d in range(8):
                here = slice(d * HALF_SEQ, (d + 1) * HALF_SEQ)
                hs = b3[here] + a3[here] * carry
                carry = hs[:, TOK - 1:TOK, :]
                out.append(hs)
            for q in range(HALF_SEQ):
                lruo_ref[l, h * HALF_SEQ + q:h * HALF_SEQ + q + 1, lanes] = carry[q]
            hs = jnp.concatenate(out, axis=0).reshape(ROWS, WID)
            hbuf[:, lanes] = (hs * gate_y).astype(BF16)
            run_ticks(t, ticks)

        loop(2, body)
        out_small(h, later(ticks, 2))

    def comp_mlp(h, m, ticks):
        base = cw.take(6)

        def body(t, _):
            slot = cw.slot(base, t)
            wait_c(slot)
            n = nbuf[h]
            gate = jax.nn.gelu(dot(n, cring[slot, 0]) + mvec[m, t, 0:1, :], approximate=True)
            up = dot(n, cring[slot, 1]) + mvec[m, t, 1:2, :]
            hbuf[:, pl.ds(pl.multiple_of(t * WID, WID), WID)] = (gate * up).astype(BF16)
            cw.refill(base, 6, t)
            run_ticks(t, ticks)

        loop(6, body)
        base_r = rw.take(8)

        def body_r(j, _):
            slot = rw.slot(base_r, j)
            wait_r(slot, 3)
            store_part(h, j, dot(hbuf[:, 0:512], rring[slot, 0]) + dot(hbuf[:, 512:1024], rring[slot, 1])
                       + dot(hbuf[:, 1024:1536], rring[slot, 2]))
            rw.refill(base_r, 8, j)
            run_ticks(j, later(ticks, 6))

        loop(8, body_r)

    def comp_att(h, l, ticks):
        for c in kv_copies(h * HALF_SEQ, 0):
            c.start()
        def row_order(ref):
            v = ref[h * HALF_SEQ:(h + 1) * HALF_SEQ].reshape(HALF_SEQ, 8, TOK, ROPE_DIM)
            return jnp.concatenate([v[q, d] for d in range(8) for q in range(HALF_SEQ)], axis=0)

        cos, sin = row_order(cos_ref), row_order(sin_ref)

        def rope(v):
            r = v[:, :ROPE_DIM]
            return jnp.concatenate([r * cos + pltpu.roll(r, ROPE_DIM // 2, 1) * sin, v[:, ROPE_DIM:]], axis=1)

        def by_seq(v):
            v = v.reshape(8, HALF_SEQ, TOK, WID)
            return [v[:, s].reshape(64, WID).astype(BF16) for s in range(HALF_SEQ)]

        n = nbuf[h]
        base = cw.take(1)
        slot = cw.slot(base, 0)
        wait_c(slot)
        for e in range(2):
            for s, v in enumerate(by_seq(rope(dot(n, cring[slot, e])))):
                qbuf[s, e * 64:(e + 1) * 64, :] = v
        cw.refill(base, 1, 0)
        run_ticks(0, ticks)
        base = cw.take(1)
        slot = cw.slot(base, 0)
        wait_c(slot)
        for s, v in enumerate(by_seq(rope(dot(n, cring[slot, 0])))):
            ko_ref[h * HALF_SEQ + s] = v
        for s, v in enumerate(by_seq(dot(n, cring[slot, 1]))):
            vo_ref[h * HALF_SEQ + s] = v
        cw.refill(base, 1, 0)
        run_ticks(0, later(ticks, 1))

        def body(s, _):
            seq = h * HALF_SEQ + s
            slot = lax.rem(s, 2)
            for c in kv_copies(seq, slot):
                c.wait()

            @pl.when(s + 1 < HALF_SEQ)
            def _():
                for c in kv_copies(seq + 1, 1 - slot):
                    c.start()

            q = qbuf[s]
            trans = (((1,), (1,)), ((), ()))
            s_old = lax.dot_general(q, kvbuf[slot, 0], trans, preferred_element_type=F32) * 0.0625
            s_new = lax.dot_general(q, ko_ref[seq], trans, preferred_element_type=F32) * 0.0625
            held = slot_ref[pl.ds(seq, 1), :]
            pos = poscol[seq]
            index = lax.rem(lax.broadcasted_iota(jnp.int32, (128, 1), 0), 64)
            last = jnp.where(pos > index, pos, -1)
            s_old = jnp.where((held >= 0) & (held <= last) & (held > pos - WINDOW), s_old, NEG)
            other = lax.broadcasted_iota(jnp.int32, (128, 64), 1)
            s_new = jnp.where((other <= index) & (other >= index - pos), s_new, NEG)
            top = jnp.maximum(row_max(s_old), row_max(s_new))
            e_old = jnp.exp(s_old - top)
            e_new = jnp.exp(s_new - top)
            inv = 1.0 / (row_sum(e_old) + row_sum(e_new))
            o = dot((e_old * inv).astype(BF16), kvbuf[slot, 1]) + dot((e_new * inv).astype(BF16), vo_ref[seq])
            o = o.reshape(2, 8, TOK, WID)
            obuf[:, s, :, 0:WID] = o[0]
            obuf[:, s, :, WID:512] = o[1]
            run_ticks(s, later(ticks, 2))

        loop(HALF_SEQ, body)
        hbuf[:, 0:512] = obuf[...].reshape(ROWS, 512).astype(BF16)
        out_small(h, later(ticks, 6))

    comp = {REC: comp_rec, MLP: comp_mlp, ATT: comp_att}

    cw.prime()
    rw.prime()
    barrier = pltpu.get_barrier_semaphore()
    for other in (sib, xn, yn):
        pl.semaphore_signal(barrier, inc=1, device_id={'tp': other}, device_id_type=pl.DeviceIdType.MESH)
    pl.semaphore_wait(barrier, 3)

    gain[...] = 1.0 + norm_ref[...].astype(F32)
    first(0)
    first(1)
    setup()

    def act(name):
        kind, i, c, h, k = name
        if kind == 'ag':
            ag_step(h, i)
        elif i == 3:
            rs3(h, k)
        else:
            (rs0, rs1, rs2)[i](h, c)

    def act_all(names):
        for name in names:
            act(name)

    after, unit = {}, None
    count = {}
    for event in plan():
        if event[0] == 'unit':
            hk = event[1:]
            unit = hk, count.get(hk, 0)
            count[hk] = unit[1] + 1
        else:
            after.setdefault(unit, []).append(event)
    act_all(after[None])
    for k, (kind, l) in enumerate(SUBLAYERS):
        for h in range(HALVES):
            last = count[h, k] - 1
            ticks = {u: (lambda names=names: act_all(names)) for (hk, u), names in
                     ((key, v) for key, v in after.items() if key) if hk == (h, k) and u < last}
            comp[kind](h, l, ticks)
            act_all(after.get(((h, k), last), ()))
    convo_ref[...] = convf[...].astype(BF16)


def update(scal_ref, new_ref, k_cache, v_cache, kn_ref, vn_ref, ko, vo, buf, in_sem, out_sem):
    pairs = [(e, q) for q in range(SEQS) for e in range(2)]

    def copy_in(e, q):
        return pltpu.make_async_copy((k_cache, v_cache)[e].at[q], buf.at[e, q], in_sem.at[e, q])

    def copy_out(e, q):
        return pltpu.make_async_copy(buf.at[e, q], (ko, vo)[e].at[q], out_sem.at[e, q])

    for e, q in pairs:
        copy_in(e, q).start()
    for e, q in pairs:
        copy_in(e, q).wait()
        for start in (pl.multiple_of(scal_ref[q], 16), 0):
            rows = pl.ds(start, SPAN)
            hit = lax.broadcasted_iota(jnp.int32, (SPAN, 64), 0) + start == new_ref[q]
            put = jnp.dot(hit.astype(BF16), (kn_ref, vn_ref)[e][q], preferred_element_type=F32)
            any_hit = row_sum(hit.astype(F32)) > 0.5
            buf[e, q, rows, :] = jnp.where(any_hit, put, buf[e, q, rows, :].astype(F32)).astype(BF16)
        copy_out(e, q).start()
    for e, q in pairs:
        copy_out(e, q).wait()


def solution(mesh):
    def device_body(x_in, seg_pos, conv_state, lru_state, k_cache, v_cache, slot_pos, norm_scale, w_x, b_x, w_y, b_y, conv_w, conv_b, w_a, b_a, w_i, b_i, a_param, w_out, b_out, w_q, w_k, w_v, w_o, b_o, w_1, b_1, w_2, b_2, w_d, b_d):
        lane = lax.broadcasted_iota(jnp.int32, (1, 1, ROPE_DIM), 2)
        half_dim = ROPE_DIM // 2
        timescale = 10000.0 ** (2.0 * (lane % half_dim).astype(F32) / ROPE_DIM)
        angle = seg_pos[:, :, None].astype(F32) / timescale
        cos = jnp.cos(angle)
        sin = jnp.where(lane < half_dim, -jnp.sin(angle), jnp.sin(angle))

        vmem = pl.BlockSpec(memory_space=pltpu.VMEM)
        hbm = pl.BlockSpec(memory_space=pl.ANY)
        sds = jax.ShapeDtypeStruct
        fresh = sds((SEQS, 64, WID), BF16)
        x_out, conv_out, lru_out, k_new, v_new = pl.pallas_call(
            mega,
            out_shape=(sds((64, D), BF16), sds((LAYERS, 3, SEQS, 512), BF16), sds((LAYERS, SEQS, 512), F32), fresh, fresh),
            in_specs=[vmem] * 22 + [hbm] * 12,
            out_specs=[vmem] * 5,
            scratch_shapes=[
                pltpu.VMEM((HALVES, ROWS, D), BF16),
                pltpu.VMEM((HALVES, NBLK, ROWS, COLS), BF16),
                pltpu.VMEM((HALVES, 4, NBLK, SHARD, COLS), BF16),
                pltpu.VMEM((HALVES, NBLK, SHARD, COLS), F32),
                pltpu.VMEM((HALVES, 3, 2, NBLK, PIECE, COLS), BF16),
                pltpu.VMEM((HALVES, 2, NBLK, PIECE, COLS), BF16),
                pltpu.VMEM((HALVES, 2, 2, NBLK, PIECE, COLS), BF16),
                pltpu.VMEM((HALVES, NBLK, SHARD, COLS), BF16),
                pltpu.VMEM((ROWS, 1536), BF16),
                pltpu.VMEM((HALF_SEQ, 128, WID), BF16),
                pltpu.VMEM((8, HALF_SEQ, TOK, 512), F32),
                pltpu.VMEM((HALVES, 2, WINDOW, WID), BF16),
                pltpu.VMEM((NC, 2, D, WID), BF16),
                pltpu.VMEM((NR, 4, 512, COLS), BF16),
                pltpu.VMEM((6, D), F32),
                pltpu.VMEM((6, D), F32),
                pltpu.VMEM((LAYERS, 2, 16, WID), F32),
                pltpu.VMEM((3, 6, 8, WID), F32),
                pltpu.VMEM((LAYERS, SEQS, TOK, 512), F32),
                pltpu.VMEM((LAYERS, 3, SEQS, 512), F32),
                pltpu.VMEM((SEQS, 128, 1), jnp.int32),
                pltpu.VMEM((HALVES, 8, HALF_SEQ, TOK, 1), jnp.int32),
                pltpu.SemaphoreType.DMA((HALVES,)),
                pltpu.SemaphoreType.DMA((HALVES, len(AG_STEPS))),
                pltpu.SemaphoreType.DMA((HALVES,)),
                pltpu.SemaphoreType.DMA((HALVES, RS_SEMS)),
                pltpu.SemaphoreType.DMA((NC, 2)),
                pltpu.SemaphoreType.DMA((NR, 4)),
                pltpu.SemaphoreType.DMA((HALVES, 2)),
            ],
            compiler_params=pltpu.CompilerParams(collective_id=0, has_side_effects=True, vmem_limit_bytes=67043328),
            name='layers',
        )(x_in.reshape(64, D), norm_scale, b_out, b_o[None], b_d, b_y, b_x, conv_w, conv_b, b_a, b_i, a_param, b_1, b_2,
          conv_state.swapaxes(1, 2), lru_state, w_a, w_i, seg_pos, slot_pos, cos, sin,
          w_y, w_x, w_out, w_1, w_2, w_d, w_q, w_k, w_v, w_o, k_cache, v_cache)

        slot_new = seg_pos & (WINDOW - 1)
        window = jnp.minimum(slot_new[:, 0] // 16 * 16, WINDOW - SPAN)
        caches = [sds(k_cache.shape, BF16)] * 2
        k_out, v_out = pl.pallas_call(
            update,
            out_shape=caches,
            in_specs=[pl.BlockSpec(memory_space=pltpu.SMEM), vmem, hbm, hbm, vmem, vmem],
            out_specs=[hbm, hbm],
            scratch_shapes=[pltpu.VMEM((2, SEQS, WINDOW, WID), BF16)] + [pltpu.SemaphoreType.DMA((2, SEQS))] * 2,
            name='caches',
        )(window, slot_new[:, None, :], k_cache, v_cache, k_new, v_new)

        first, last = seg_pos[:, :1], seg_pos[:, 63:]
        count = jnp.where(last < 63, 63 - last, 64)
        slot = lax.broadcasted_iota(jnp.int32, (1, WINDOW), 1)
        ahead = (slot - first) & (WINDOW - 1)
        slot_out = jnp.where(ahead < count, first + ahead, jnp.where(slot < 64 - count, slot, slot_pos))
        return x_out.reshape(8, 8, D), conv_out.swapaxes(1, 2), lru_out, k_out, v_out, slot_out

    col_spec = P(None, None, 'tp')
    vec_spec = P(None, 'tp')
    row_spec = vec_spec
    x_spec, seq_spec, conv_spec, lru_spec = P('dp', 'tp'), P('dp'), P(None, 'dp', None, 'tp'), P(None, 'dp', 'tp')
    arg_specs = (x_spec, seq_spec, conv_spec, lru_spec, seq_spec, seq_spec, seq_spec, P(), col_spec, vec_spec, col_spec, vec_spec, col_spec, vec_spec, row_spec, vec_spec, row_spec, vec_spec, vec_spec, row_spec, P(), vec_spec, P(), P(), P('tp'), P(), col_spec, vec_spec, col_spec, vec_spec, row_spec, P())
    result_specs = (x_spec, conv_spec, lru_spec, seq_spec, seq_spec, seq_spec)
    return jax.shard_map(device_body, mesh=mesh, in_specs=arg_specs, out_specs=result_specs, check_vma=False)
```

time: 925 us -> 283 us (0.31); the launches traced: 911 us -> 282 us
  waiting for transfers between devices: 388 us -> 0 us
  local copies, waits for them, and re-layouts: 283 us -> 4.16 us
  Pallas kernels: 0 us -> 273 us
  matrix products: 168 us -> 0 us
  other arithmetic: 53.6 us -> 4.64 us
  between operations: 16.1 us -> 0.68 us
    pallas_call x0 -> x2, Pallas kernels: none -> 273 us  [the longest x1 260 us: device_body(): pl.pallas_call(mega, out_shape=(sds((64, D), BF16), sds((LAYERS, 3, SEQS,...]
    unnamed x18 -> x0, waiting for transfers between devices: 210 us -> none
    all_gather x6 -> x0, waiting for transfers between devices: 178 us -> none  [gather_tokens(): return lax.all_gather(normed_loc, 'tp', axis=1, tiled=True)]
    dot_general x22 -> x0, matrix products: 168 us -> none  [the longest x14 154 us: linear_map(): jnp.einsum('bcd,df->bcf', act_in, weight, preferred_element_type=jnp.floa...]
    scatter x3 -> x0, local copies, waits for them, and re-layouts: 150 us -> none  [the longest x1 63 us: attention_local(): v_out = v_cache.at[batch_idx, slot_new].set(value_new, unique_indices=True)]
    unnamed x157 -> x13, local copies, waits for them, and re-layouts: 55.4 us -> 2.05 us
    slice x69 -> x1, local copies, waits for them, and re-layouts: 50 us -> 0.8 us  [device_body(): window = jnp.minimum(slot_new[:, 0] // 16 * 16, WINDOW - SPAN)]
    pad x20 -> x0, local copies, waits for them, and re-layouts: 22.2 us -> none  [recurrent_local(): lax.associative_scan(lru_combine, (decay_a, drive_in), axis=1)[1]]
  transfers between devices with their start and end apart: 12 -> 0, of which waited for: 11 -> 0; matrix products, arithmetic and copies ran while one was open for 18% -> 0% of each run, Pallas kernels for 0% -> 0%
where the time goes in v1:
time: 283 us; the launch traced here: 282 us
  Pallas kernels  273 us (96%)
  other arithmetic  4.64 us (2%)
  local copies, waits for them, and re-layouts  4.16 us (1%)
    pallas_call x1, Pallas kernels, device_body(): pl.pallas_call(mega, out_shape=(sds((64, D), BF16), sds((LAYERS, 3, SEQS,...  260 us
    pallas_call x1, Pallas kernels, device_body(): pl.pallas_call(update, out_shape=caches, in_specs=[pl.BlockSpec(memory_sp...  13.2 us

profile of v1, /device:TPU:0, one launch (start us, length us, event | category | flops | bytes accessed | tf_op | source)
XLA Modules:
  0.0 282.3 jit_solution(13440913110507653596)
XLA Ops:
  0.6 1.3 broadcast_in_dim.25.bo_ref
  2.0 1.4 broadcast_and_fusion
  3.3 1.8 negate_select_fusion
  5.1 259.6 %layers.1 = (bf16[64,4096]{1,0:T(8,128)(2,1)}, bf16[2,3,8,512]{3,2,1,0:T(8,128)(2,1)}, f32[2,8,512]{2,1,0:T(8,128)}, bf16[8,64,256]{2,1,0:T(8,128)(2,1)}, bf16[8,64,256]{2,1,0:T(8,128)(2,1)}) custom-call(bf16[64,4096]{1,0:T(8,128)(2,1)} %bitcast.5, bf16[6,4096]{1,0:T(8,128)(2,1)} %norm_ref.1, bf16[2,4096]{1,0:T(2,128)(2,1)} %bout_ref.1, ...), custom_call_target="tpu_custom_call" | custom-call | tf_op jit(solution)/shard_map/layers/pallas_call | solution.py:689
  264.7 0.8 slice_reduce_fusion.1
  265.5 0.5 multiply_minimum_fusion.scal_ref
  266.1 0.0 copy-start.2
  266.1 0.0 copy-start.1
  266.1 0.0 copy-start
  266.1 0.0 copy-start.3
  266.1 0.0 copy-start.4
  266.1 13.2 %caches.1 = (bf16[8,2048,256]{2,1,0:T(8,128)(2,1)}, bf16[8,2048,256]{2,1,0:T(8,128)(2,1)}) custom-call(s32[8]{0:T(128)} %multiply_minimum_fusion.scal_ref, s32[8,1,64]{2,1,0:T(1,128)} %bitcast.9, bf16[8,2048,256]{2,1,0:T(8,128)(2,1)} %k_cache.3, bf16[8,2048,256]{2,1,0:T(8,128)(2,1)} %v_cache.3, bf16[8,64,256]{2,1,0:T(8,128)(2,1)} %get-tuple-element.16.kn_ref, ...), custom_call_target="tpu_custom_call" | custom-call | tf_op jit(solution)/shard_map/caches/pallas_call | solution.py:734
  279.3 0.0 copy-done.2
  279.3 0.2 slice_reduce_fusion
  279.5 0.0 copy-done.1
  279.5 0.7 select_select_fusion
  280.2 0.0 copy-done
  280.2 0.8 copy.41
  281.0 0.0 copy-done.3
  281.0 0.6 copy.42
  281.7 0.0 copy-done.4
  281.7 0.6 copy.43
  (2 shorter events, 0.0 us)
Async XLA Ops:
  266.1 13.2 %copy-start.2 = (s32[8,64]{1,0:T(8,128)S(1)}, s32[8,64]{1,0:T(8,128)}, u32[]{:S(2)}) copy-start(s32[8,64]{1,0:T(8,128)} %pos_ref.1) | copy-start | bytes 6148
  266.1 13.4 %copy-start.1 = (s32[8,2048]{1,0:T(8,128)S(1)}, s32[8,2048]{1,0:T(8,128)}, u32[]{:S(2)}) copy-start(s32[8,2048]{1,0:T(8,128)} %slot_ref.1) | copy-start | bytes 196612
  266.1 14.2 %copy-start = (bf16[64,4096]{1,0:T(8,128)(2,1)S(1)}, bf16[64,4096]{1,0:T(8,128)(2,1)}, u32[]{:S(2)}) copy-start(bf16[64,4096]{1,0:T(8,128)(2,1)} %get-tuple-element.13) | copy-start | bytes 1572868
  266.1 15.0 %copy-start.3 = (bf16[2,3,8,512]{3,2,1,0:T(8,128)(2,1)S(1)}, bf16[2,3,8,512]{3,2,1,0:T(8,128)(2,1)}, u32[]{:S(2)}) copy-start(bf16[2,3,8,512]{3,2,1,0:T(8,128)(2,1)} %get-tuple-element.14) | copy-start | bytes 147460
  266.1 15.6 %copy-start.4 = (f32[2,8,512]{2,1,0:T(8,128)S(1)}, f32[2,8,512]{2,1,0:T(8,128)}, u32[]{:S(2)}) copy-start(f32[2,8,512]{2,1,0:T(8,128)} %get-tuple-element.35) | copy-start | bytes 98308

commit v2 on v1

--- a/solution.py
+++ b/solution.py
@@ -28,6 +28,7 @@
 REC, MLP, ATT = 'rec', 'mlp', 'att'
 SUBLAYERS = ((REC, 0), (MLP, 0), (REC, 1), (MLP, 1), (ATT, 0), (MLP, 2))
 
+UNITS = {REC: 4, MLP: 10, ATT: 8}
 AG_OWN = ('x0', 'y1', 'x1', 'y0', 'so')
 AG_STEPS = (
     (('x0', 'y1'), ('dy0', 'dx1', 'sx0', 'sy1')),
@@ -43,85 +44,28 @@
 RS_SEMS = 3 * CHUNKS + 1
 RS_ORDER = ((0, 0), (1, 0), (0, 1), (1, 1), (2, 0), (2, 1))
 
-UNITS = {REC: (2, 2.4, 2, 0.6), MLP: (6, 1.4, 8, 0.6), ATT: (6, 1.7, 2, 0.6)}
-LINK_US, D2D_US, LINK_LATENCY, D2D_LATENCY = 2.81, 0.22, 1.9, 1.0
-
-
-def link_of(name):
-    if name[0] == 's':
-        return 's'
-    return 'x' if name in ('x0', 'x1', 'dx1', 'd0') else 'y'
+PLAN = (
+    'aabaa.b..bab.aab.aa..babaa.bbaabba...b....b.a..aababab..',
+    'a..a....ab.b.ababba...ab.aaaaabbabbb.a..ba.bbaba.b..b..b',
+    '....ba.aabbaab..a..a....ab..bbbaaba.b..b...b.a.aabbaab..',
+    'a..a...a.bbbbaaba..b..b....ab.a.babaab........ba..bbbbab',
+    'b',
+)
 
 
 def plan():
-    free = dict.fromkeys('xys', 0.0)
-    ends = {}
-    now = 0.0
-
-    def send(key, size):
-        link = link_of(key[-1])
-        rate, latency = (D2D_US, D2D_LATENCY) if link == 's' else (LINK_US, LINK_LATENCY)
-        free[link] = max(now, free[link]) + size * rate
-        ends[key] = free[link] + latency
-
-    def own(h, k):
-        for name in AG_OWN:
-            send((h, k, 'g', name), 2 if name == 'so' else 1)
-
     def chain(h):
-        steps = []
-        for k, (kind, _) in enumerate(SUBLAYERS):
-            n_col, _, n_row, _ = UNITS[kind]
-            for i, (waits, sends) in enumerate(AG_STEPS):
-                steps.append((('ag', i, 0, h, k), 0, [(h, k, 'g', w) for w in waits], [((h, k, 'g', w), 1) for w in sends], 0))
+        if h:
+            yield 'start', 0, 0, h, 0
+        for k in range(len(SUBLAYERS)):
+            for i in range(len(AG_STEPS)):
+                yield 'ag', i, 0, h, k
             for step, c in RS_ORDER:
-                need = n_col + n_row * (c + 1) // CHUNKS if step == 0 else 0
-                waits = ((), ('s3', 's1', 's2', 's0'), ('d0', 'd1'))[step]
-                sends = (('s3', 's1', 's2', 's0'), ('d0', 'd1', 'x0', 'y1'), ('y0', 'x1'))[step]
-                steps.append((('rs', step, c, h, k), need, [(h, k, c, w) for w in waits],
-                              [((h, k, c, w), (2 if step == 0 else 1) / CHUNKS) for w in sends], 0.15))
-            steps.append((('rs', 3, 0, h, k), 0, [(h, k, c, w) for c in range(CHUNKS) for w in RS_IN], [], 0.7))
-        return steps
-
-    waiting = [chain(0), chain(1)]
-    computing = [(h, k) for k in range(len(SUBLAYERS)) for h in range(2)]
-    unit, done, gathered, order = 0, {}, set(), []
-    own(0, 0)
-    own(1, 0)
-    while waiting[0] or waiting[1]:
-        heads = []
-        for h in range(2):
-            if waiting[h]:
-                step = waiting[h][0]
-                if done.get((h, step[0][-1]), 0) >= step[1]:
-                    heads.append((max([ends[w] for w in step[2]], default=0.0), step[0][-1], h))
-        ready = [(k, h) for t, k, h in heads if t <= now]
-        if not ready and computing and computing[0] in gathered:
-            h, k = computing[0]
-            n_col, col_us, n_row, row_us = UNITS[SUBLAYERS[k][0]]
-            now += col_us if unit < n_col else row_us
-            order.append(('unit', h, k))
-            unit += 1
-            done[h, k] = unit
-            if unit == n_col + n_row:
-                computing.pop(0)
-                unit = 0
-            continue
-        if ready:
-            h = min(ready)[1]
-        else:
-            now, _, h = min(heads)
-        name, _, _, sends, us = waiting[h].pop(0)
-        k = name[-1]
-        now += us
-        for key, size in sends:
-            send(key, size)
-        if name[:2] == ('ag', 3):
-            gathered.add((h, k))
-        if name[:2] == ('rs', 3) and k + 1 < len(SUBLAYERS):
-            own(h, k + 1)
-        order.append(name)
-    return order
+                yield 'rs', step, c, h, k
+            yield 'rs', 3, 0, h, k
+
+    ahead = {'a': chain(0), 'b': chain(1)}
+    return [next(ahead[c]) if c in ahead else None for c in ''.join(PLAN)]
 
 
 class Ring:
@@ -520,15 +464,18 @@
         loop(6, body)
         base_r = rw.take(8)
 
-        def body_r(j, _):
-            slot = rw.slot(base_r, j)
-            wait_r(slot, 3)
-            store_part(h, j, dot(hbuf[:, 0:512], rring[slot, 0]) + dot(hbuf[:, 512:1024], rring[slot, 1])
-                       + dot(hbuf[:, 1024:1536], rring[slot, 2]))
-            rw.refill(base_r, 8, j)
-            run_ticks(j, later(ticks, 6))
-
-        loop(8, body_r)
+        def body_r(i, _):
+            for e in range(2):
+                wait_r(rw.slot(base_r, 2 * i + e), 3)
+            for e in range(2):
+                slot = rw.slot(base_r, 2 * i + e)
+                store_part(h, 2 * i + e, dot(hbuf[:, 0:512], rring[slot, 0]) + dot(hbuf[:, 512:1024], rring[slot, 1])
+                           + dot(hbuf[:, 1024:1536], rring[slot, 2]))
+            for e in range(2):
+                rw.refill(base_r, 8, 2 * i + e)
+            run_ticks(i, later(ticks, 6))
+
+        loop(4, body_r)
 
     def comp_att(h, l, ticks):
         for c in kv_copies(h * HALF_SEQ, 0):
@@ -613,12 +560,13 @@
 
     gain[...] = 1.0 + norm_ref[...].astype(F32)
     first(0)
-    first(1)
     setup()
 
     def act(name):
         kind, i, c, h, k = name
-        if kind == 'ag':
+        if kind == 'start':
+            first(h)
+        elif kind == 'ag':
             ag_step(h, i)
         elif i == 3:
             rs3(h, k)
@@ -629,23 +577,22 @@
         for name in names:
             act(name)
 
-    after, unit = {}, None
-    count = {}
+    after, unit = {-1: []}, -1
     for event in plan():
-        if event[0] == 'unit':
-            hk = event[1:]
-            unit = hk, count.get(hk, 0)
-            count[hk] = unit[1] + 1
+        if event is None:
+            unit += 1
+            after[unit] = []
         else:
-            after.setdefault(unit, []).append(event)
-    act_all(after[None])
+            after[unit].append(event)
+    act_all(after[-1])
+    base = 0
     for k, (kind, l) in enumerate(SUBLAYERS):
         for h in range(HALVES):
-            last = count[h, k] - 1
-            ticks = {u: (lambda names=names: act_all(names)) for (hk, u), names in
-                     ((key, v) for key, v in after.items() if key) if hk == (h, k) and u < last}
+            last = base + UNITS[kind] - 1
+            ticks = {u - base: (lambda names=after[u]: act_all(names)) for u in range(base, last) if after[u]}
             comp[kind](h, l, ticks)
-            act_all(after.get(((h, k), last), ()))
+            act_all(after[last])
+            base = last + 1
     convo_ref[...] = convf[...].astype(BF16)
 
 

time: 283 us -> 263 us (0.929)
  Pallas kernels: 273 us -> 254 us
    pallas_call x1, Pallas kernels: 260 us -> 240 us  [device_body(): pl.pallas_call(mega, out_shape=(sds((64, D), BF16), sds((LAYERS, 3, SEQS,...]
where the time goes in v2:
time: 263 us
  Pallas kernels  254 us (97%)
  other arithmetic  4.64 us (2%)
  local copies, waits for them, and re-layouts  4.16 us (2%)
    pallas_call x1, Pallas kernels, device_body(): pl.pallas_call(mega, out_shape=(sds((64, D), BF16), sds((LAYERS, 3, SEQS,...  240 us
    pallas_call x1, Pallas kernels, device_body(): pl.pallas_call(update, out_shape=caches, in_specs=[pl.BlockSpec(memory_sp...  13.2 us

profile of v2, /device:TPU:0, one launch (start us, length us, event | category | flops | bytes accessed | tf_op | source)
XLA Modules:
  0.0 263.0 jit_solution(5409869215940870514)
XLA Ops:
  0.6 1.3 broadcast_in_dim.25.bo_ref
  2.0 1.4 broadcast_and_fusion
  3.3 1.8 negate_select_fusion
  5.1 240.3 %layers.1 = (bf16[64,4096]{1,0:T(8,128)(2,1)}, bf16[2,3,8,512]{3,2,1,0:T(8,128)(2,1)}, f32[2,8,512]{2,1,0:T(8,128)}, bf16[8,64,256]{2,1,0:T(8,128)(2,1)}, bf16[8,64,256]{2,1,0:T(8,128)(2,1)}) custom-call(bf16[64,4096]{1,0:T(8,128)(2,1)} %bitcast.5, bf16[6,4096]{1,0:T(8,128)(2,1)} %norm_ref.1, bf16[2,4096]{1,0:T(2,128)(2,1)} %bout_ref.1, ...), custom_call_target="tpu_custom_call" | custom-call | tf_op jit(solution)/shard_map/layers/pallas_call | solution.py:636
  245.5 0.8 slice_reduce_fusion.1
  246.3 0.5 multiply_minimum_fusion.scal_ref
  246.8 0.0 copy-start.2
  246.8 0.0 copy-start.1
  246.8 0.0 copy-start
  246.8 0.0 copy-start.3
  246.8 0.0 copy-start.4
  246.8 13.2 %caches.1 = (bf16[8,2048,256]{2,1,0:T(8,128)(2,1)}, bf16[8,2048,256]{2,1,0:T(8,128)(2,1)}) custom-call(s32[8]{0:T(128)} %multiply_minimum_fusion.scal_ref, s32[8,1,64]{2,1,0:T(1,128)} %bitcast.9, bf16[8,2048,256]{2,1,0:T(8,128)(2,1)} %k_cache.3, bf16[8,2048,256]{2,1,0:T(8,128)(2,1)} %v_cache.3, bf16[8,64,256]{2,1,0:T(8,128)(2,1)} %get-tuple-element.16.kn_ref, ...), custom_call_target="tpu_custom_call" | custom-call | tf_op jit(solution)/shard_map/caches/pallas_call | solution.py:681
  260.0 0.0 copy-done.2
  260.0 0.2 slice_reduce_fusion
  260.2 0.0 copy-done.1
  260.2 0.7 select_select_fusion
  261.0 0.0 copy-done
  261.0 0.8 copy.41
  261.8 0.0 copy-done.3
  261.8 0.6 copy.42
  262.4 0.0 copy-done.4
  262.4 0.6 copy.43
  (2 shorter events, 0.0 us)
Async XLA Ops:
  246.8 13.2 %copy-start.2 = (s32[8,64]{1,0:T(8,128)S(1)}, s32[8,64]{1,0:T(8,128)}, u32[]{:S(2)}) copy-start(s32[8,64]{1,0:T(8,128)} %pos_ref.1) | copy-start | bytes 6148
  246.8 13.4 %copy-start.1 = (s32[8,2048]{1,0:T(8,128)S(1)}, s32[8,2048]{1,0:T(8,128)}, u32[]{:S(2)}) copy-start(s32[8,2048]{1,0:T(8,128)} %slot_ref.1) | copy-start | bytes 196612
  246.8 14.2 %copy-start = (bf16[64,4096]{1,0:T(8,128)(2,1)S(1)}, bf16[64,4096]{1,0:T(8,128)(2,1)}, u32[]{:S(2)}) copy-start(bf16[64,4096]{1,0:T(8,128)(2,1)} %get-tuple-element.13) | copy-start | bytes 1572868
  246.8 15.0 %copy-start.3 = (bf16[2,3,8,512]{3,2,1,0:T(8,128)(2,1)S(1)}, bf16[2,3,8,512]{3,2,1,0:T(8,128)(2,1)}, u32[]{:S(2)}) copy-start(bf16[2,3,8,512]{3,2,1,0:T(8,128)(2,1)} %get-tuple-element.14) | copy-start | bytes 147460
  246.8 15.6 %copy-start.4 = (f32[2,8,512]{2,1,0:T(8,128)S(1)}, f32[2,8,512]{2,1,0:T(8,128)}, u32[]{:S(2)}) copy-start(f32[2,8,512]{2,1,0:T(8,128)} %get-tuple-element.35) | copy-start | bytes 98308

commit v3 on v2

--- a/solution.py
+++ b/solution.py
@@ -29,27 +29,16 @@
 SUBLAYERS = ((REC, 0), (MLP, 0), (REC, 1), (MLP, 1), (ATT, 0), (MLP, 2))
 
 UNITS = {REC: 4, MLP: 10, ATT: 8}
-AG_OWN = ('x0', 'y1', 'x1', 'y0', 'so')
-AG_STEPS = (
-    (('x0', 'y1'), ('dy0', 'dx1', 'sx0', 'sy1')),
-    (('x1', 'y0'), ('sx1', 'sy0')),
-    (('dy0', 'dx1'), ('sd0', 'sd1')),
-    (('so', 'sx0', 'sy1', 'sx1', 'sy0', 'sd0', 'sd1'), ()),
-)
-AG_STEP_OF = {name: i for i, (waits, _) in enumerate(AG_STEPS) for name in waits}
-AG_ROWS = tuple(sum(SHARD if name == 'so' else PIECE for name in waits) for waits, _ in AG_STEPS)
-RS_IN = ('x0', 'y1', 'x1', 'y0')
-CHUNKS = 2
-CBLK = NBLK // CHUNKS
-RS_SEMS = 3 * CHUNKS + 1
-RS_ORDER = ((0, 0), (1, 0), (0, 1), (1, 1), (2, 0), (2, 1))
+STEPS = (('ag', 1, 0), ('ag', 2, 0), ('ag', 1, 1), ('ag', 2, 1), ('ag', 3, 0), ('ag', 3, 1), ('ag', 4, 0),
+         ('rs', 0, 0), ('rs', 1, 0), ('rs', 0, 1), ('rs', 1, 1), ('rs', 2, 0), ('rs', 2, 1), ('rs', 3, 0), ('rs', 3, 1))
+HALF_BLK = NBLK // 2
 
 PLAN = (
-    'aabaa.b..bab.aab.aa..babaa.bbaabba...b....b.a..aababab..',
-    'a..a....ab.b.ababba...ab.aaaaabbabbb.a..ba.bbaba.b..b..b',
-    '....ba.aabbaab..a..a....ab..bbbaaba.b..b...b.a.aabbaab..',
-    'a..a...a.bbbbaaba..b..b....ab.a.babaab........ba..bbbbab',
-    'b',
+    'aaaaabaa...ab.bbaabbabb.a.a.baa.bbaaaabaaab..b.b..b..b.a',
+    'bb..aabbbab..a..a.a..a.ab..bbaabaaaab.bb.b.a.bbaabbabbba',
+    '.aa.a.b.aabbabaaaab..b.b..b.b.b.ab..aabbbab..a..a.a..a.b',
+    '.a.bbaabaaaab...bb..b..ab.bbaababbb.a..a.a.a..baa.bbaaba',
+    'aab..b.b..b.b..abb.b.baabab........ba..bbabaabbbb',
 )
 
 
@@ -58,11 +47,8 @@
         if h:
             yield 'start', 0, 0, h, 0
         for k in range(len(SUBLAYERS)):
-            for i in range(len(AG_STEPS)):
-                yield 'ag', i, 0, h, k
-            for step, c in RS_ORDER:
-                yield 'rs', step, c, h, k
-            yield 'rs', 3, 0, h, k
+            for step in STEPS:
+                yield *step, h, k
 
     ahead = {'a': chain(0), 'b': chain(1)}
     return [next(ahead[c]) if c in ahead else None for c in ''.join(PLAN)]
@@ -116,7 +102,7 @@
 
 
 def sum_blocks(body):
-    return lax.fori_loop(0, NBLK, body, jnp.zeros((SHARD, COLS), F32))
+    return lax.fori_loop(0, NBLK, body, jnp.zeros((PIECE, COLS), F32))
 
 
 def row_sum(v):
@@ -218,58 +204,64 @@
             return pl.ds(pl.multiple_of(SHARD * dev, SHARD), SHARD)
         return pl.ds(pl.multiple_of(SHARD * dev + PIECE * p, PIECE), PIECE)
 
-    def ag(h, name):
-        p = None if name == 'so' else int(name[-1])
-        origin = {'so': me, 'x': me, 'y': me, 'dy': xn, 'dx': yn, 'sx': xn, 'sy': yn, 'sd': dg}[name if name == 'so' else name[:-1]]
-        target = sib if name[0] == 's' else xn if name in ('x0', 'x1', 'dx1') else yn
-        ref = nbuf.at[h, rows_of(origin, p), :]
-        return pltpu.make_async_remote_copy(src_ref=ref, dst_ref=ref, send_sem=ag_s.at[h], recv_sem=ag_r.at[h, AG_STEP_OF[name]],
-                                            device_id={'tp': target}, device_id_type=pl.DeviceIdType.MESH)
-
-    def ag0(h):
-        for name in AG_OWN:
-            ag(h, name).start()
-
-    def ag_step(h, i):
-        waits, sends = AG_STEPS[i]
-        await_bytes(nbuf.at[h, pl.ds(0, AG_ROWS[i]), :], ag_r.at[h, i])
-        for name in sends:
-            ag(h, name).start()
-        if i == 3:
-            await_bytes(nbuf.at[h, pl.ds(0, sum(AG_ROWS)), :], ag_s.at[h])
+    def ag(h, what, r, part=None):
+        origin = {'x': me, 'y': me, 'so': me, 'dy': xn, 'dx': yn, 'sx': xn, 'sy': yn, 'sd': dg}[what]
+        target = sib if what[0] == 's' else xn if what[-1] == 'x' else yn
+        sem = 6 if part is None else 4 + r if what[0] == 'd' else 2 * r + (part if what == 'x' else 1 - part)
+        ref = nbuf.at[h, rows_of(origin, r), :] if part is None else nbuf.at[h, rows_of(origin, r), pl.ds(part * D // 2, D // 2)]
+        pltpu.make_async_remote_copy(src_ref=ref, dst_ref=ref, send_sem=ag_s.at[h], recv_sem=ag_r.at[h, sem],
+                                     device_id={'tp': target}, device_id_type=pl.DeviceIdType.MESH).start()
+
+    def ag_own(h, r):
+        ag(h, 'x', r, 0)
+        ag(h, 'y', r, 1)
+        ag(h, 'x', r, 1)
+        ag(h, 'y', r, 0)
+        ag(h, 'so', r)
+
+    def ag_step(h, i, r):
+        sem = (2 * r, 2 * r + 1, 4 + r, 6)[i - 1]
+        await_bytes(nbuf.at[h, pl.ds(0, 8 * PIECE if i == 4 else PIECE), :], ag_r.at[h, sem])
+        if i == 1:
+            ag(h, 'dy', r, 0)
+            ag(h, 'dx', r, 1)
+        elif i == 2:
+            ag(h, 'sx', r)
+            ag(h, 'sy', r)
+        elif i == 3:
+            ag(h, 'sd', r)
+        else:
+            await_bytes(nbuf.at[h, pl.ds(0, ROWS - SHARD), :], ag_s.at[h])
 
     chip_rows = (me, xn, yn, dg)
     other_rows = (sib, xn + 1 - 2 * core, yn + 1 - 2 * core, dg + 1 - 2 * core)
 
-    def rs_sem(name, c):
-        if name in RS_IN:
-            return RS_SEMS - 1
-        return c * 3 + (0 if name == 's3' else 1 if name[0] == 's' else 2)
-
-    def rs(h, name, c):
-        p = int(name[1])
-        cb = pl.ds(c * CBLK, CBLK)
-        if name[0] == 's':
-            src, dst, target = part.at[h, cb, rows_of(other_rows[p]), :], sibr.at[h, p, cb], sib
-        elif name[0] == 'd':
-            src, dst, target = tbuf.at[h, 2, p, cb], dgr.at[h, p, cb], (xn if p == 0 else yn)
-        elif name[0] == 'x':
-            src, dst, target = tbuf.at[h, 0, p, cb], xyr.at[h, 0, p, cb], xn
+    def remote(h, src, dst, sem, target):
+        pltpu.make_async_remote_copy(src_ref=src, dst_ref=dst, send_sem=rs_s.at[h], recv_sem=rs_r.at[h, sem],
+                                     device_id={'tp': target}, device_id_type=pl.DeviceIdType.MESH).start()
+
+    def half_blks(c):
+        return pl.ds(c * HALF_BLK, HALF_BLK)
+
+    def rs(h, what, r, c):
+        cb = half_blks(c)
+        if what == 'd':
+            remote(h, tbuf.at[h, 2, r, cb], dgr.at[h, r, cb], 2 + r, yn if c else xn)
         else:
-            src, dst, target = tbuf.at[h, 1, p, cb], xyr.at[h, 1, p, cb], yn
-        return pltpu.make_async_remote_copy(src_ref=src, dst_ref=dst, send_sem=rs_s.at[h], recv_sem=rs_r.at[h, rs_sem(name, c)],
-                                            device_id={'tp': target}, device_id_type=pl.DeviceIdType.MESH)
+            to = 0 if what == 'x' else 1
+            remote(h, tbuf.at[h, to, r, cb], xyr.at[h, to, r, cb], 4 + r, yn if to else xn)
 
     def rs0(h, c):
+        cb = half_blks(c)
         for p in (3, 1, 2, 0):
-            rs(h, 's%d' % p, c).start()
+            remote(h, part.at[h, cb, rows_of(other_rows[p]), :], sibr.at[h, p, cb], c, sib)
 
     def rs1(h, c):
-        cb = pl.ds(c * CBLK, CBLK)
-
-        def some(p):
-            def body(i, _):
-                j = c * CBLK + i
+        await_bytes(sibr.at[h, :, half_blks(c)], rs_r.at[h, c])
+
+        def body(i, _):
+            j = c * HALF_BLK + i
+            for p in range(4):
                 v = part[h, j, rows_of(chip_rows[p]), :].astype(F32) + sibr[h, p, j].astype(F32)
                 if p == 0:
                     town[h, j] = v
@@ -278,72 +270,74 @@
                     tbuf[h, p - 1, 0, j] = v[:PIECE]
                     tbuf[h, p - 1, 1, j] = v[PIECE:]
 
-            loop(CBLK, body)
-
-        await_bytes(sibr.at[h, 3, cb], rs_r.at[h, rs_sem('s3', c)])
-        some(3)
-        rs(h, 'd0', c).start()
-        rs(h, 'd1', c).start()
-        await_bytes(sibr.at[h, pl.ds(0, 3), cb], rs_r.at[h, rs_sem('s0', c)])
-        some(1)
-        rs(h, 'x0', c).start()
-        some(2)
-        rs(h, 'y1', c).start()
-        some(0)
-
-    def rs2(h, c):
-        await_bytes(dgr.at[h, :, pl.ds(c * CBLK, CBLK)], rs_r.at[h, rs_sem('d0', c)])
+        loop(HALF_BLK, body)
+        if c == 1:
+            rs(h, 'd', 0, 0)
+            rs(h, 'd', 0, 1)
+            rs(h, 'x', 0, 0)
+            rs(h, 'y', 0, 1)
+            rs(h, 'd', 1, 0)
+            rs(h, 'd', 1, 1)
+
+    def rs2(h, r):
+        await_bytes(dgr.at[h, r], rs_r.at[h, 2 + r])
 
         def body(i, _):
-            j = c * CBLK + i
-            for to, p in ((1, 0), (0, 1)):
-                tbuf[h, to, p, j] = (tbuf[h, to, p, j].astype(F32) + dgr[h, p, j].astype(F32)).astype(BF16)
-
-        loop(CBLK, body)
-        rs(h, 'y0', c).start()
-        rs(h, 'x1', c).start()
+            for to, j in ((1, i), (0, HALF_BLK + i)):
+                tbuf[h, to, r, j] = (tbuf[h, to, r, j].astype(F32) + dgr[h, r, j].astype(F32)).astype(BF16)
+
+        loop(HALF_BLK, body)
+        rs(h, 'x', r, 1)
+        rs(h, 'y', r, 0)
+        if r == 0:
+            rs(h, 'x', 1, 0)
+            rs(h, 'y', 1, 1)
 
     def blk(j):
         return pl.ds(pl.multiple_of(j * COLS, COLS), COLS)
 
-    def normalise(h, k, square_sum):
+    def normalise(h, k, r, square_sum):
         inv = lax.rsqrt(row_sum(square_sum) * (1.0 / D) + 1e-6)
 
         def body(j, _):
-            nbuf[h, rows_of(me), blk(j)] = (xres[h, j].astype(F32) * inv * gain[k:k + 1, blk(j)]).astype(BF16)
+            nbuf[h, rows_of(me, r), blk(j)] = (xres[h, r, j].astype(F32) * inv * gain[k:k + 1, blk(j)]).astype(BF16)
 
         loop(NBLK, body)
+        ag_own(h, r)
 
     def first(h):
+        for r in range(2):
+            def body(j, acc):
+                row = h * SHARD + r * PIECE
+                v = x_ref[row:row + PIECE, blk(j)]
+                xres[h, r, j] = v
+                v = v.astype(F32)
+                return acc + v * v
+
+            normalise(h, 0, r, sum_blocks(body))
+
+    def rs3(h, k, r):
+        await_bytes(xyr.at[h, :, r], rs_r.at[h, 4 + r])
+        last = k == len(SUBLAYERS) - 1
+        here = slice(r * PIECE, (r + 1) * PIECE)
+
         def body(j, acc):
-            v = x_ref[h * SHARD:(h + 1) * SHARD, blk(j)]
-            xres[h, j] = v
+            got = xyr[h, 0, r, j].astype(F32) + xyr[h, 1, r, j].astype(F32)
+            v = xres[h, r, j].astype(F32) + (town[h, j, here] + got) + bias[k:k + 1, blk(j)]
+            v = v.astype(BF16)
+            if last:
+                row = h * SHARD + r * PIECE
+                xo_ref[row:row + PIECE, blk(j)] = v
+                return acc
+            xres[h, r, j] = v
             v = v.astype(F32)
             return acc + v * v
 
-        normalise(h, 0, sum_blocks(body))
-        ag0(h)
-
-    def rs3(h, k):
-        await_bytes(xyr.at[h], rs_r.at[h, RS_SEMS - 1])
-        last = k == len(SUBLAYERS) - 1
-
-        def body(j, acc):
-            got = jnp.concatenate([xyr[h, 0, p, j].astype(F32) + xyr[h, 1, p, j].astype(F32) for p in range(2)], axis=0)
-            v = xres[h, j].astype(F32) + (town[h, j] + got) + bias[k:k + 1, blk(j)]
-            v = v.astype(BF16)
-            if last:
-                xo_ref[h * SHARD:(h + 1) * SHARD, blk(j)] = v
-                return acc
-            xres[h, j] = v
-            v = v.astype(F32)
-            return acc + v * v
-
         square_sum = sum_blocks(body)
-        await_bytes(part.at[h, :, pl.ds(0, ROWS - SHARD), :], rs_s.at[h])
+        if r == 1:
+            await_bytes(part.at[h, :, pl.ds(0, ROWS - SHARD), :], rs_s.at[h])
         if not last:
-            normalise(h, k + 1, square_sum)
-            ag0(h)
+            normalise(h, k + 1, r, square_sum)
 
     def setup():
         for k, (ref, l) in enumerate(((bout_ref, 0), (bd_ref, 0), (bout_ref, 1), (bd_ref, 1), (bo_ref, 0), (bd_ref, 2))):
@@ -567,9 +561,9 @@
         if kind == 'start':
             first(h)
         elif kind == 'ag':
-            ag_step(h, i)
+            ag_step(h, i, c)
         elif i == 3:
-            rs3(h, k)
+            rs3(h, k, c)
         else:
             (rs0, rs1, rs2)[i](h, c)
 
@@ -646,7 +640,7 @@
                 pltpu.VMEM((HALVES, 3, 2, NBLK, PIECE, COLS), BF16),
                 pltpu.VMEM((HALVES, 2, NBLK, PIECE, COLS), BF16),
                 pltpu.VMEM((HALVES, 2, 2, NBLK, PIECE, COLS), BF16),
-                pltpu.VMEM((HALVES, NBLK, SHARD, COLS), BF16),
+                pltpu.VMEM((HALVES, 2, NBLK, PIECE, COLS), BF16),
                 pltpu.VMEM((ROWS, 1536), BF16),
                 pltpu.VMEM((HALF_SEQ, 128, WID), BF16),
                 pltpu.VMEM((8, HALF_SEQ, TOK, 512), F32),
@@ -662,9 +656,9 @@
                 pltpu.VMEM((SEQS, 128, 1), jnp.int32),
                 pltpu.VMEM((HALVES, 8, HALF_SEQ, TOK, 1), jnp.int32),
                 pltpu.SemaphoreType.DMA((HALVES,)),
-                pltpu.SemaphoreType.DMA((HALVES, len(AG_STEPS))),
+                pltpu.SemaphoreType.DMA((HALVES, 7)),
                 pltpu.SemaphoreType.DMA((HALVES,)),
-                pltpu.SemaphoreType.DMA((HALVES, RS_SEMS)),
+                pltpu.SemaphoreType.DMA((HALVES, 6)),
                 pltpu.SemaphoreType.DMA((NC, 2)),
                 pltpu.SemaphoreType.DMA((NR, 4)),
                 pltpu.SemaphoreType.DMA((HALVES, 2)),

time: 263 us -> 255 us (0.970)
  Pallas kernels: 254 us -> 246 us
    pallas_call x1, Pallas kernels: 240 us -> 232 us  [device_body(): pl.pallas_call(mega, out_shape=(sds((64, D), BF16), sds((LAYERS, 3, SEQS,...]
where the time goes in v3:
time: 255 us
  Pallas kernels  246 us (96%)
  other arithmetic  4.64 us (2%)
  local copies, waits for them, and re-layouts  4.16 us (2%)
    pallas_call x1, Pallas kernels, device_body(): pl.pallas_call(mega, out_shape=(sds((64, D), BF16), sds((LAYERS, 3, SEQS,...  232 us
    pallas_call x1, Pallas kernels, device_body(): pl.pallas_call(update, out_shape=caches, in_specs=[pl.BlockSpec(memory_sp...  13.2 us

profile of v3, /device:TPU:0, one launch (start us, length us, event | category | flops | bytes accessed | tf_op | source)
XLA Modules:
  0.0 255.1 jit_solution(5318764063902304953)
XLA Ops:
  0.6 1.3 broadcast_in_dim.25.bo_ref
  2.0 1.4 broadcast_and_fusion
  3.3 1.8 negate_select_fusion
  5.1 232.4 %layers.1 = (bf16[64,4096]{1,0:T(8,128)(2,1)}, bf16[2,3,8,512]{3,2,1,0:T(8,128)(2,1)}, f32[2,8,512]{2,1,0:T(8,128)}, bf16[8,64,256]{2,1,0:T(8,128)(2,1)}, bf16[8,64,256]{2,1,0:T(8,128)(2,1)}) custom-call(bf16[64,4096]{1,0:T(8,128)(2,1)} %bitcast.5, bf16[6,4096]{1,0:T(8,128)(2,1)} %norm_ref.1, bf16[2,4096]{1,0:T(2,128)(2,1)} %bout_ref.1, ...), custom_call_target="tpu_custom_call" | custom-call | tf_op jit(solution)/shard_map/layers/pallas_call | solution.py:630
  237.5 0.8 slice_reduce_fusion.1
  238.3 0.5 multiply_minimum_fusion.scal_ref
  238.9 0.0 copy-start.2
  238.9 0.0 copy-start.1
  238.9 0.0 copy-start
  238.9 0.0 copy-start.3
  238.9 0.0 copy-start.4
  238.9 13.2 %caches.1 = (bf16[8,2048,256]{2,1,0:T(8,128)(2,1)}, bf16[8,2048,256]{2,1,0:T(8,128)(2,1)}) custom-call(s32[8]{0:T(128)} %multiply_minimum_fusion.scal_ref, s32[8,1,64]{2,1,0:T(1,128)} %bitcast.9, bf16[8,2048,256]{2,1,0:T(8,128)(2,1)} %k_cache.3, bf16[8,2048,256]{2,1,0:T(8,128)(2,1)} %v_cache.3, bf16[8,64,256]{2,1,0:T(8,128)(2,1)} %get-tuple-element.16.kn_ref, ...), custom_call_target="tpu_custom_call" | custom-call | tf_op jit(solution)/shard_map/caches/pallas_call | solution.py:675
  252.1 0.0 copy-done.2
  252.1 0.2 slice_reduce_fusion
  252.3 0.0 copy-done.1
  252.3 0.7 select_select_fusion
  253.0 0.0 copy-done
  253.0 0.8 copy.41
  253.8 0.0 copy-done.3
  253.8 0.6 copy.42
  254.4 0.0 copy-done.4
  254.5 0.6 copy.43
  (2 shorter events, 0.0 us)
Async XLA Ops:
  238.9 13.2 %copy-start.2 = (s32[8,64]{1,0:T(8,128)S(1)}, s32[8,64]{1,0:T(8,128)}, u32[]{:S(2)}) copy-start(s32[8,64]{1,0:T(8,128)} %pos_ref.1) | copy-start | bytes 6148
  238.9 13.4 %copy-start.1 = (s32[8,2048]{1,0:T(8,128)S(1)}, s32[8,2048]{1,0:T(8,128)}, u32[]{:S(2)}) copy-start(s32[8,2048]{1,0:T(8,128)} %slot_ref.1) | copy-start | bytes 196612
  238.9 14.2 %copy-start = (bf16[64,4096]{1,0:T(8,128)(2,1)S(1)}, bf16[64,4096]{1,0:T(8,128)(2,1)}, u32[]{:S(2)}) copy-start(bf16[64,4096]{1,0:T(8,128)(2,1)} %get-tuple-element.13) | copy-start | bytes 1572868
  238.9 15.0 %copy-start.3 = (bf16[2,3,8,512]{3,2,1,0:T(8,128)(2,1)S(1)}, bf16[2,3,8,512]{3,2,1,0:T(8,128)(2,1)}, u32[]{:S(2)}) copy-start(bf16[2,3,8,512]{3,2,1,0:T(8,128)(2,1)} %get-tuple-element.14) | copy-start | bytes 147460
  238.9 15.6 %copy-start.4 = (f32[2,8,512]{2,1,0:T(8,128)S(1)}, f32[2,8,512]{2,1,0:T(8,128)}, u32[]{:S(2)}) copy-start(f32[2,8,512]{2,1,0:T(8,128)} %get-tuple-element.35) | copy-start | bytes 98308

commit v4 on v3

--- a/solution.py
+++ b/solution.py
@@ -340,8 +340,9 @@
             normalise(h, k + 1, r, square_sum)
 
     def setup():
-        for k, (ref, l) in enumerate(((bout_ref, 0), (bd_ref, 0), (bout_ref, 1), (bd_ref, 1), (bo_ref, 0), (bd_ref, 2))):
-            bias[k:k + 1, :] = ref[...].astype(F32)[l:l + 1]
+        for k, (ref, l) in enumerate(((bout_ref, 0), (bd_ref, 0), (bout_ref, 1), (bd_ref, 1), (bo_ref, None), (bd_ref, 2))):
+            v = ref[...].astype(F32)
+            bias[k:k + 1, :] = v.reshape(1, D) if l is None else v[l:l + 1]
         rows = [(by_ref[...], 1), (bx_ref[...], 1)] + [(cw_ref[:, i], 1) for i in range(4)]
         rows += [(cb_ref[...], 1), (ba_ref[...], 1), (bi_ref[...], 1), (jax.nn.softplus(ap_ref[...]), -8.0)]
         for r, (v, scale) in enumerate(rows):
@@ -590,7 +591,8 @@
     convo_ref[...] = convf[...].astype(BF16)
 
 
-def update(scal_ref, new_ref, k_cache, v_cache, kn_ref, vn_ref, ko, vo, buf, in_sem, out_sem):
+def finish(pos_s, pos_ref, slot_ref, k_cache, v_cache, kn_ref, vn_ref, x_ref, conv_ref, lru_ref,
+           ko, vo, so_ref, xo_ref, convo_ref, lruo_ref, buf, in_sem, out_sem):
     pairs = [(e, q) for q in range(SEQS) for e in range(2)]
 
     def copy_in(e, q):
@@ -601,15 +603,28 @@
 
     for e, q in pairs:
         copy_in(e, q).start()
-    for e, q in pairs:
-        copy_in(e, q).wait()
-        for start in (pl.multiple_of(scal_ref[q], 16), 0):
+    xo_ref[...] = x_ref[...]
+    convo_ref[...] = conv_ref[...]
+    lruo_ref[...] = lru_ref[...]
+    begin, last = pos_ref[:, 0:1], pos_ref[:, 63:64]
+    count = jnp.where(last < 63, 63 - last, 64)
+    slot = lax.broadcasted_iota(jnp.int32, (SEQS, WINDOW), 1)
+    ahead = (slot - begin) & (WINDOW - 1)
+    so_ref[...] = jnp.where(ahead < count, begin + ahead, jnp.where(slot < 64 - count, slot, slot_ref[...]))
+    for q in range(SEQS):
+        first_row = pl.multiple_of(jnp.minimum((pos_s[q, 0] & (WINDOW - 1)) // PIECE * PIECE, WINDOW - SPAN), PIECE)
+        new_slots = pos_ref[q:q + 1, :] & (WINDOW - 1)
+        for e in range(2):
+            copy_in(e, q).wait()
+        for start in (first_row, 0):
             rows = pl.ds(start, SPAN)
-            hit = lax.broadcasted_iota(jnp.int32, (SPAN, 64), 0) + start == new_ref[q]
-            put = jnp.dot(hit.astype(BF16), (kn_ref, vn_ref)[e][q], preferred_element_type=F32)
+            hit = lax.broadcasted_iota(jnp.int32, (SPAN, 64), 0) + start == new_slots
             any_hit = row_sum(hit.astype(F32)) > 0.5
-            buf[e, q, rows, :] = jnp.where(any_hit, put, buf[e, q, rows, :].astype(F32)).astype(BF16)
-        copy_out(e, q).start()
+            for e, ref in enumerate((kn_ref, vn_ref)):
+                put = jnp.dot(hit.astype(BF16), ref[q], preferred_element_type=F32)
+                buf[e, q, rows, :] = jnp.where(any_hit, put, buf[e, q, rows, :].astype(F32)).astype(BF16)
+        for e in range(2):
+            copy_out(e, q).start()
     for e, q in pairs:
         copy_out(e, q).wait()
 
@@ -665,28 +680,19 @@
             ],
             compiler_params=pltpu.CompilerParams(collective_id=0, has_side_effects=True, vmem_limit_bytes=67043328),
             name='layers',
-        )(x_in.reshape(64, D), norm_scale, b_out, b_o[None], b_d, b_y, b_x, conv_w, conv_b, b_a, b_i, a_param, b_1, b_2,
+        )(x_in.reshape(64, D), norm_scale, b_out, b_o, b_d, b_y, b_x, conv_w, conv_b, b_a, b_i, a_param, b_1, b_2,
           conv_state.swapaxes(1, 2), lru_state, w_a, w_i, seg_pos, slot_pos, cos, sin,
           w_y, w_x, w_out, w_1, w_2, w_d, w_q, w_k, w_v, w_o, k_cache, v_cache)
 
-        slot_new = seg_pos & (WINDOW - 1)
-        window = jnp.minimum(slot_new[:, 0] // 16 * 16, WINDOW - SPAN)
-        caches = [sds(k_cache.shape, BF16)] * 2
-        k_out, v_out = pl.pallas_call(
-            update,
-            out_shape=caches,
-            in_specs=[pl.BlockSpec(memory_space=pltpu.SMEM), vmem, hbm, hbm, vmem, vmem],
-            out_specs=[hbm, hbm],
+        k_out, v_out, slot_out, x_out, conv_out, lru_out = pl.pallas_call(
+            finish,
+            out_shape=[sds(v.shape, v.dtype) for v in (k_cache, v_cache, slot_pos, x_out, conv_out, lru_out)],
+            in_specs=[pl.BlockSpec(memory_space=pltpu.SMEM), vmem, vmem, hbm, hbm] + [vmem] * 5,
+            out_specs=[hbm, hbm] + [vmem] * 4,
             scratch_shapes=[pltpu.VMEM((2, SEQS, WINDOW, WID), BF16)] + [pltpu.SemaphoreType.DMA((2, SEQS))] * 2,
             name='caches',
-        )(window, slot_new[:, None, :], k_cache, v_cache, k_new, v_new)
-
-        first, last = seg_pos[:, :1], seg_pos[:, 63:]
-        count = jnp.where(last < 63, 63 - last, 64)
-        slot = lax.broadcasted_iota(jnp.int32, (1, WINDOW), 1)
-        ahead = (slot - first) & (WINDOW - 1)
-        slot_out = jnp.where(ahead < count, first + ahead, jnp.where(slot < 64 - count, slot, slot_pos))
-        return x_out.reshape(8, 8, D), conv_out.swapaxes(1, 2), lru_out, k_out, v_out, slot_out
+        )(seg_pos, seg_pos, slot_pos, k_cache, v_cache, k_new, v_new, x_out, conv_out, lru_out)
+        return x_out.reshape(SEQS, TOK, D), conv_out.swapaxes(1, 2), lru_out, k_out, v_out, slot_out
 
     col_spec = P(None, None, 'tp')
     vec_spec = P(None, 'tp')

time: 255 us -> 250 us (0.980)
  local copies, waits for them, and re-layouts: 4.16 us -> 0 us
where the time goes in v4:
time: 250 us
  Pallas kernels  247 us (99%)
  other arithmetic  2.51 us (1%)
    pallas_call x1, Pallas kernels, device_body(): pl.pallas_call(mega, out_shape=(sds((64, D), BF16), sds((LAYERS, 3, SEQS,...  232 us
    pallas_call x1, Pallas kernels, device_body(): pl.pallas_call(finish, out_shape=[sds(v.shape, v.dtype) for v in (k_cache...  14.3 us

profile of v4, /device:TPU:0, one launch (start us, length us, event | category | flops | bytes accessed | tf_op | source)
XLA Modules:
  0.0 250.1 jit_solution(18165652171563720282)
XLA Ops:
  0.7 0.7 convert_element_type.12
  1.3 1.8 negate_select_fusion
  3.2 232.4 %layers.1 = (bf16[64,4096]{1,0:T(8,128)(2,1)}, bf16[2,3,8,512]{3,2,1,0:T(8,128)(2,1)}, f32[2,8,512]{2,1,0:T(8,128)}, bf16[8,64,256]{2,1,0:T(8,128)(2,1)}, bf16[8,64,256]{2,1,0:T(8,128)(2,1)}) custom-call(bf16[64,4096]{1,0:T(8,128)(2,1)} %bitcast.4, bf16[6,4096]{1,0:T(8,128)(2,1)} %norm_ref.1, bf16[2,4096]{1,0:T(2,128)(2,1)} %bout_ref.1, ...), custom_call_target="tpu_custom_call" | custom-call | tf_op jit(solution)/shard_map/layers/pallas_call | solution.py:645
  235.6 14.3 %caches.1 = (bf16[8,2048,256]{2,1,0:T(8,128)(2,1)}, bf16[8,2048,256]{2,1,0:T(8,128)(2,1)}, s32[8,2048]{1,0:T(8,128)}, bf16[64,4096]{1,0:T(8,128)(2,1)}, bf16[2,3...) custom-call(s32[8,64]{1,0:T(8,128)} %pos_ref.3, s32[8,64]{1,0:T(8,128)} %pos_ref.3, s32[8,2048]{1,0:T(8,128)} %slot_ref.3, ...), custom_call_target="tpu_custom_call" | custom-call | tf_op jit(solution)/shard_map/caches/pallas_call | solution.py:687
  (2 shorter events, 0.0 us)

commit v5 on v4

--- a/solution.py
+++ b/solution.py
@@ -22,6 +22,8 @@
 WID = 256
 HALVES = LAYERS = 2
 SEQS = 8
+TOKENS = 64
+BIG = 1 << 30
 SPAN = 96
 NEG = -1e30
 
@@ -127,11 +129,11 @@
 
 
 def mega(x_ref, norm_ref, bout_ref, bo_ref, bd_ref, by_ref, bx_ref, cw_ref, cb_ref, ba_ref, bi_ref, ap_ref, b1_ref, b2_ref,
-         conv_ref, lru_ref, wa_ref, wi_ref, pos_ref, slot_ref, cos_ref, sin_ref,
+         conv_ref, lru_ref, wa_ref, wi_ref, pos_ref, slot_ref, scale_ref,
          w_y, w_x, w_out, w_1, w_2, w_d, w_q, w_k, w_v, w_o, k_cache, v_cache,
          xo_ref, convo_ref, lruo_ref, ko_ref, vo_ref,
          nbuf, part, sibr, town, tbuf, dgr, xyr, xres, hbuf, qbuf, obuf, kvbuf, cring, rring,
-         gain, bias, rvec, mvec, conv0, convf, poscol, posrow,
+         gain, bias, rvec, mvec, conv0, convf, poscol, posrow, costab, sintab,
          ag_s, ag_r, rs_s, rs_r, csem, rsem, kvsem):
     me = lax.axis_index('tp')
     core = lax.rem(me, 2)
@@ -254,26 +256,33 @@
     def rs0(h, c):
         cb = half_blks(c)
         for p in (3, 1, 2, 0):
-            remote(h, part.at[h, cb, rows_of(other_rows[p]), :], sibr.at[h, p, cb], c, sib)
+            remote(h, part.at[h, cb, rows_of(other_rows[p]), :], sibr.at[h, p, cb], 6 + c if p == 3 else c, sib)
 
     def rs1(h, c):
-        await_bytes(sibr.at[h, :, half_blks(c)], rs_r.at[h, c])
-
-        def body(i, _):
-            j = c * HALF_BLK + i
-            for p in range(4):
-                v = part[h, j, rows_of(chip_rows[p]), :].astype(F32) + sibr[h, p, j].astype(F32)
-                if p == 0:
-                    town[h, j] = v
-                else:
-                    v = v.astype(BF16)
-                    tbuf[h, p - 1, 0, j] = v[:PIECE]
-                    tbuf[h, p - 1, 1, j] = v[PIECE:]
-
-        loop(HALF_BLK, body)
+        cb = half_blks(c)
+
+        def add_up(kinds):
+            def body(i, _):
+                j = c * HALF_BLK + i
+                for p in kinds:
+                    v = part[h, j, rows_of(chip_rows[p]), :].astype(F32) + sibr[h, p, j].astype(F32)
+                    if p == 0:
+                        town[h, j] = v
+                    else:
+                        v = v.astype(BF16)
+                        tbuf[h, p - 1, 0, j] = v[:PIECE]
+                        tbuf[h, p - 1, 1, j] = v[PIECE:]
+
+            loop(HALF_BLK, body)
+
+        await_bytes(sibr.at[h, 3, cb], rs_r.at[h, 6 + c])
+        add_up((3,))
         if c == 1:
             rs(h, 'd', 0, 0)
             rs(h, 'd', 0, 1)
+        await_bytes(sibr.at[h, pl.ds(0, 3), cb], rs_r.at[h, c])
+        add_up((1, 2, 0))
+        if c == 1:
             rs(h, 'x', 0, 0)
             rs(h, 'y', 0, 1)
             rs(h, 'd', 1, 0)
@@ -365,8 +374,14 @@
         cols = jnp.concatenate([p, p], axis=1).T
         for q in range(SEQS):
             col = cols[:, q:q + 1]
-            poscol[q] = col
-            posrow[q // HALF_SEQ, :, q % HALF_SEQ] = col[:64].reshape(8, TOK, 1)
+            poscol[q] = col[:TOKENS]
+            posrow[q // HALF_SEQ, :, q % HALF_SEQ] = col[:TOKENS].reshape(8, TOK, 1)
+        lane = lax.broadcasted_iota(jnp.int32, (1, ROPE_DIM), 1)
+        for h in range(HALVES):
+            angle = posrow[h].reshape(ROWS, 1).astype(F32) / scale_ref[...]
+            costab[h] = jnp.cos(angle)
+            sine = jnp.sin(angle)
+            sintab[h] = jnp.where(lane < ROPE_DIM // 2, -sine, sine)
 
     def dot(a, b):
         return jnp.dot(a, b, preferred_element_type=F32)
@@ -475,11 +490,7 @@
     def comp_att(h, l, ticks):
         for c in kv_copies(h * HALF_SEQ, 0):
             c.start()
-        def row_order(ref):
-            v = ref[h * HALF_SEQ:(h + 1) * HALF_SEQ].reshape(HALF_SEQ, 8, TOK, ROPE_DIM)
-            return jnp.concatenate([v[q, d] for d in range(8) for q in range(HALF_SEQ)], axis=0)
-
-        cos, sin = row_order(cos_ref), row_order(sin_ref)
+        cos, sin = costab[h], sintab[h]
 
         def rope(v):
             r = v[:, :ROPE_DIM]
@@ -487,15 +498,15 @@
 
         def by_seq(v):
             v = v.reshape(8, HALF_SEQ, TOK, WID)
-            return [v[:, s].reshape(64, WID).astype(BF16) for s in range(HALF_SEQ)]
+            return [v[:, s].reshape(TOKENS, WID).astype(BF16) for s in range(HALF_SEQ)]
 
         n = nbuf[h]
         base = cw.take(1)
         slot = cw.slot(base, 0)
         wait_c(slot)
         for e in range(2):
-            for s, v in enumerate(by_seq(rope(dot(n, cring[slot, e])))):
-                qbuf[s, e * 64:(e + 1) * 64, :] = v
+            for s, v in enumerate(by_seq(rope(dot(n, cring[slot, e])) * 0.0625)):
+                qbuf[s, e * TOKENS:(e + 1) * TOKENS, :] = v
         cw.refill(base, 1, 0)
         run_ticks(0, ticks)
         base = cw.take(1)
@@ -521,15 +532,18 @@
 
             q = qbuf[s]
             trans = (((1,), (1,)), ((), ()))
-            s_old = lax.dot_general(q, kvbuf[slot, 0], trans, preferred_element_type=F32) * 0.0625
-            s_new = lax.dot_general(q, ko_ref[seq], trans, preferred_element_type=F32) * 0.0625
+            s_old = lax.dot_general(q, kvbuf[slot, 0], trans, preferred_element_type=F32)
+            s_new = lax.dot_general(q, ko_ref[seq], trans, preferred_element_type=F32)
             held = slot_ref[pl.ds(seq, 1), :]
+            held = jnp.where(held >= 0, held, BIG)
             pos = poscol[seq]
-            index = lax.rem(lax.broadcasted_iota(jnp.int32, (128, 1), 0), 64)
+            index = lax.broadcasted_iota(jnp.int32, (TOKENS, 1), 0)
             last = jnp.where(pos > index, pos, -1)
-            s_old = jnp.where((held >= 0) & (held <= last) & (held > pos - WINDOW), s_old, NEG)
-            other = lax.broadcasted_iota(jnp.int32, (128, 64), 1)
-            s_new = jnp.where((other <= index) & (other >= index - pos), s_new, NEG)
+            seen = (held <= last) & (held > pos - WINDOW)
+            s_old = jnp.where(seen[None], s_old.reshape(2, TOKENS, WINDOW), NEG).reshape(128, WINDOW)
+            other = lax.broadcasted_iota(jnp.int32, (TOKENS, TOKENS), 1)
+            seen = (other <= index) & (other >= index - pos)
+            s_new = jnp.where(seen[None], s_new.reshape(2, TOKENS, TOKENS), NEG).reshape(128, TOKENS)
             top = jnp.maximum(row_max(s_old), row_max(s_new))
             e_old = jnp.exp(s_old - top)
             e_new = jnp.exp(s_new - top)
@@ -592,7 +606,7 @@
 
 
 def finish(pos_s, pos_ref, slot_ref, k_cache, v_cache, kn_ref, vn_ref, x_ref, conv_ref, lru_ref,
-           ko, vo, so_ref, xo_ref, convo_ref, lruo_ref, buf, in_sem, out_sem):
+           ko, vo, so_ref, xo_ref, convo_ref, lruo_ref, buf, xbuf, cbuf, lbuf, in_sem, out_sem, small_in, small_out):
     pairs = [(e, q) for q in range(SEQS) for e in range(2)]
 
     def copy_in(e, q):
@@ -603,14 +617,17 @@
 
     for e, q in pairs:
         copy_in(e, q).start()
-    xo_ref[...] = x_ref[...]
-    convo_ref[...] = conv_ref[...]
-    lruo_ref[...] = lru_ref[...]
-    begin, last = pos_ref[:, 0:1], pos_ref[:, 63:64]
-    count = jnp.where(last < 63, 63 - last, 64)
+    small = ((x_ref, xbuf, xo_ref), (conv_ref, cbuf, convo_ref), (lru_ref, lbuf, lruo_ref))
+    for i, (src, mid, _) in enumerate(small):
+        pltpu.make_async_copy(src, mid, small_in.at[i]).start()
+    begin, last = pos_ref[:, 0:1], pos_ref[:, 63:TOKENS]
+    count = jnp.where(last < 63, 63 - last, TOKENS)
     slot = lax.broadcasted_iota(jnp.int32, (SEQS, WINDOW), 1)
     ahead = (slot - begin) & (WINDOW - 1)
-    so_ref[...] = jnp.where(ahead < count, begin + ahead, jnp.where(slot < 64 - count, slot, slot_ref[...]))
+    so_ref[...] = jnp.where(ahead < count, begin + ahead, jnp.where(slot < TOKENS - count, slot, slot_ref[...]))
+    for i, (src, mid, dst) in enumerate(small):
+        pltpu.make_async_copy(src, mid, small_in.at[i]).wait()
+        pltpu.make_async_copy(mid, dst, small_out.at[i]).start()
     for q in range(SEQS):
         first_row = pl.multiple_of(jnp.minimum((pos_s[q, 0] & (WINDOW - 1)) // PIECE * PIECE, WINDOW - SPAN), PIECE)
         new_slots = pos_ref[q:q + 1, :] & (WINDOW - 1)
@@ -618,7 +635,7 @@
             copy_in(e, q).wait()
         for start in (first_row, 0):
             rows = pl.ds(start, SPAN)
-            hit = lax.broadcasted_iota(jnp.int32, (SPAN, 64), 0) + start == new_slots
+            hit = lax.broadcasted_iota(jnp.int32, (SPAN, TOKENS), 0) + start == new_slots
             any_hit = row_sum(hit.astype(F32)) > 0.5
             for e, ref in enumerate((kn_ref, vn_ref)):
                 put = jnp.dot(hit.astype(BF16), ref[q], preferred_element_type=F32)
@@ -627,25 +644,23 @@
             copy_out(e, q).start()
     for e, q in pairs:
         copy_out(e, q).wait()
+    for i, (_, mid, dst) in enumerate(small):
+        pltpu.make_async_copy(mid, dst, small_out.at[i]).wait()
 
 
 def solution(mesh):
     def device_body(x_in, seg_pos, conv_state, lru_state, k_cache, v_cache, slot_pos, norm_scale, w_x, b_x, w_y, b_y, conv_w, conv_b, w_a, b_a, w_i, b_i, a_param, w_out, b_out, w_q, w_k, w_v, w_o, b_o, w_1, b_1, w_2, b_2, w_d, b_d):
-        lane = lax.broadcasted_iota(jnp.int32, (1, 1, ROPE_DIM), 2)
         half_dim = ROPE_DIM // 2
-        timescale = 10000.0 ** (2.0 * (lane % half_dim).astype(F32) / ROPE_DIM)
-        angle = seg_pos[:, :, None].astype(F32) / timescale
-        cos = jnp.cos(angle)
-        sin = jnp.where(lane < half_dim, -jnp.sin(angle), jnp.sin(angle))
+        timescale = 10000.0 ** (2.0 * (jnp.arange(ROPE_DIM) % half_dim).astype(F32) / ROPE_DIM)
 
         vmem = pl.BlockSpec(memory_space=pltpu.VMEM)
         hbm = pl.BlockSpec(memory_space=pl.ANY)
         sds = jax.ShapeDtypeStruct
-        fresh = sds((SEQS, 64, WID), BF16)
+        fresh = sds((SEQS, TOKENS, WID), BF16)
         x_out, conv_out, lru_out, k_new, v_new = pl.pallas_call(
             mega,
-            out_shape=(sds((64, D), BF16), sds((LAYERS, 3, SEQS, 512), BF16), sds((LAYERS, SEQS, 512), F32), fresh, fresh),
-            in_specs=[vmem] * 22 + [hbm] * 12,
+            out_shape=(sds((TOKENS, D), BF16), sds((LAYERS, 3, SEQS, 512), BF16), sds((LAYERS, SEQS, 512), F32), fresh, fresh),
+            in_specs=[vmem] * 21 + [hbm] * 12,
             out_specs=[vmem] * 5,
             scratch_shapes=[
                 pltpu.VMEM((HALVES, ROWS, D), BF16),
@@ -668,28 +683,31 @@
                 pltpu.VMEM((3, 6, 8, WID), F32),
                 pltpu.VMEM((LAYERS, SEQS, TOK, 512), F32),
                 pltpu.VMEM((LAYERS, 3, SEQS, 512), F32),
-                pltpu.VMEM((SEQS, 128, 1), jnp.int32),
+                pltpu.VMEM((SEQS, TOKENS, 1), jnp.int32),
                 pltpu.VMEM((HALVES, 8, HALF_SEQ, TOK, 1), jnp.int32),
+                pltpu.VMEM((HALVES, ROWS, ROPE_DIM), F32),
+                pltpu.VMEM((HALVES, ROWS, ROPE_DIM), F32),
                 pltpu.SemaphoreType.DMA((HALVES,)),
                 pltpu.SemaphoreType.DMA((HALVES, 7)),
                 pltpu.SemaphoreType.DMA((HALVES,)),
-                pltpu.SemaphoreType.DMA((HALVES, 6)),
+                pltpu.SemaphoreType.DMA((HALVES, 8)),
                 pltpu.SemaphoreType.DMA((NC, 2)),
                 pltpu.SemaphoreType.DMA((NR, 4)),
                 pltpu.SemaphoreType.DMA((HALVES, 2)),
             ],
             compiler_params=pltpu.CompilerParams(collective_id=0, has_side_effects=True, vmem_limit_bytes=67043328),
             name='layers',
-        )(x_in.reshape(64, D), norm_scale, b_out, b_o, b_d, b_y, b_x, conv_w, conv_b, b_a, b_i, a_param, b_1, b_2,
-          conv_state.swapaxes(1, 2), lru_state, w_a, w_i, seg_pos, slot_pos, cos, sin,
+        )(x_in.reshape(TOKENS, D), norm_scale, b_out, b_o, b_d, b_y, b_x, conv_w, conv_b, b_a, b_i, a_param, b_1, b_2,
+          conv_state.swapaxes(1, 2), lru_state, w_a, w_i, seg_pos, slot_pos, timescale[None],
           w_y, w_x, w_out, w_1, w_2, w_d, w_q, w_k, w_v, w_o, k_cache, v_cache)
 
         k_out, v_out, slot_out, x_out, conv_out, lru_out = pl.pallas_call(
             finish,
             out_shape=[sds(v.shape, v.dtype) for v in (k_cache, v_cache, slot_pos, x_out, conv_out, lru_out)],
-            in_specs=[pl.BlockSpec(memory_space=pltpu.SMEM), vmem, vmem, hbm, hbm] + [vmem] * 5,
-            out_specs=[hbm, hbm] + [vmem] * 4,
-            scratch_shapes=[pltpu.VMEM((2, SEQS, WINDOW, WID), BF16)] + [pltpu.SemaphoreType.DMA((2, SEQS))] * 2,
+            in_specs=[pl.BlockSpec(memory_space=pltpu.SMEM), vmem, vmem, hbm, hbm, vmem, vmem] + [hbm] * 3,
+            out_specs=[hbm, hbm, vmem] + [hbm] * 3,
+            scratch_shapes=[pltpu.VMEM((2, SEQS, WINDOW, WID), BF16)] + [pltpu.VMEM(v.shape, v.dtype) for v in (x_out, conv_out, lru_out)]
+            + [pltpu.SemaphoreType.DMA((2, SEQS))] * 2 + [pltpu.SemaphoreType.DMA((3,))] * 2,
             name='caches',
         )(seg_pos, seg_pos, slot_pos, k_cache, v_cache, k_new, v_new, x_out, conv_out, lru_out)
         return x_out.reshape(SEQS, TOK, D), conv_out.swapaxes(1, 2), lru_out, k_out, v_out, slot_out

time: 250 us -> 246 us (0.984)
  no operation moved by 1% of the time
where the time goes in v5:
time: 246 us
  Pallas kernels  245 us (100%)
    pallas_call x1, Pallas kernels, device_body(): pl.pallas_call(mega, out_shape=(sds((TOKENS, D), BF16), sds((LAYERS, 3, S...  231 us
    pallas_call x1, Pallas kernels, device_body(): pl.pallas_call(finish, out_shape=[sds(v.shape, v.dtype) for v in (k_cache...  13.9 us

profile of v5, /device:TPU:0, one launch (start us, length us, event | category | flops | bytes accessed | tf_op | source)
XLA Modules:
  0.0 246.2 jit_solution(15222855256964159617)
XLA Ops:
  0.6 0.5 fusion.2.scale_ref
  1.2 231.0 %layers.1 = (bf16[64,4096]{1,0:T(8,128)(2,1)}, bf16[2,3,8,512]{3,2,1,0:T(8,128)(2,1)}, f32[2,8,512]{2,1,0:T(8,128)}, bf16[8,64,256]{2,1,0:T(8,128)(2,1)}, bf16[8,64,256]{2,1,0:T(8,128)(2,1)}) custom-call(bf16[64,4096]{1,0:T(8,128)(2,1)} %bitcast.4, bf16[6,4096]{1,0:T(8,128)(2,1)} %norm_ref.1, bf16[2,4096]{1,0:T(2,128)(2,1)} %bout_ref.1, ...), custom_call_target="tpu_custom_call" | custom-call | tf_op jit(solution)/shard_map/layers/pallas_call | solution.py:660
  232.1 13.9 %caches.1 = (bf16[8,2048,256]{2,1,0:T(8,128)(2,1)}, bf16[8,2048,256]{2,1,0:T(8,128)(2,1)}, s32[8,2048]{1,0:T(8,128)}, bf16[64,4096]{1,0:T(8,128)(2,1)}, bf16[2,3...) custom-call(s32[8,64]{1,0:T(8,128)} %pos_ref.3, s32[8,64]{1,0:T(8,128)} %pos_ref.3, s32[8,2048]{1,0:T(8,128)} %slot_ref.3, ...), custom_call_target="tpu_custom_call" | custom-call | tf_op jit(solution)/shard_map/caches/pallas_call | solution.py:704

commit v6 on v5

--- a/solution.py
+++ b/solution.py
@@ -36,11 +36,11 @@
 HALF_BLK = NBLK // 2
 
 PLAN = (
-    'aaaaabaa...ab.bbaabbabb.a.a.baa.bbaaaabaaab..b.b..b..b.a',
-    'bb..aabbbab..a..a.a..a.ab..bbaabaaaab.bb.b.a.bbaabbabbba',
-    '.aa.a.b.aabbabaaaab..b.b..b.b.b.ab..aabbbab..a..a.a..a.b',
-    '.a.bbaabaaaab...bb..b..ab.bbaababbb.a..a.a.a..baa.bbaaba',
-    'aab..b.b..b.b..abb.b.baabab........ba..bbabaabbbb',
+    'aaaaabaa...abb.bbaababba.aa.a.abba.babaaaab..b.b..b..b.a',
+    'b.b.aabbabb.a..a.a..a.a.b.a.abbbaaaab.bb.bb.a.baabbabbab',
+    '.aa.a.ba.abababaaab..b.b..b.b..a.bb.aabbabb.a..a.a..a..b',
+    'a.a.abbabaaab...bb..b..abb.baaabbbba...aa..a..b.aaabbbaa',
+    'aab..b.b..b..b.abb.b.ababab....a....ba..bbbbababb',
 )
 
 

time: 246 us -> 246 us (level)
  no operation moved by 1% of the time
where the time goes in v6:
time: 246 us; the launch traced here: 245 us
  Pallas kernels  244 us (99%)
    pallas_call x1, Pallas kernels, device_body(): pl.pallas_call(mega, out_shape=(sds((TOKENS, D), BF16), sds((LAYERS, 3, S...  230 us
    pallas_call x1, Pallas kernels, device_body(): pl.pallas_call(finish, out_shape=[sds(v.shape, v.dtype) for v in (k_cache...  13.9 us

profile of v6, /device:TPU:0, one launch (start us, length us, event | category | flops | bytes accessed | tf_op | source)
XLA Modules:
  0.0 245.4 jit_solution(13565301786350520197)
XLA Ops:
  0.6 0.5 fusion.2.scale_ref
  1.2 230.2 %layers.1 = (bf16[64,4096]{1,0:T(8,128)(2,1)}, bf16[2,3,8,512]{3,2,1,0:T(8,128)(2,1)}, f32[2,8,512]{2,1,0:T(8,128)}, bf16[8,64,256]{2,1,0:T(8,128)(2,1)}, bf16[8,64,256]{2,1,0:T(8,128)(2,1)}) custom-call(bf16[64,4096]{1,0:T(8,128)(2,1)} %bitcast.4, bf16[6,4096]{1,0:T(8,128)(2,1)} %norm_ref.1, bf16[2,4096]{1,0:T(2,128)(2,1)} %bout_ref.1, ...), custom_call_target="tpu_custom_call" | custom-call | tf_op jit(solution)/shard_map/layers/pallas_call | solution.py:660
  231.3 13.9 %caches.1 = (bf16[8,2048,256]{2,1,0:T(8,128)(2,1)}, bf16[8,2048,256]{2,1,0:T(8,128)(2,1)}, s32[8,2048]{1,0:T(8,128)}, bf16[64,4096]{1,0:T(8,128)(2,1)}, bf16[2,3...) custom-call(s32[8,64]{1,0:T(8,128)} %pos_ref.3, s32[8,64]{1,0:T(8,128)} %pos_ref.3, s32[8,2048]{1,0:T(8,128)} %slot_ref.3, ...), custom_call_target="tpu_custom_call" | custom-call | tf_op jit(solution)/shard_map/caches/pallas_call | solution.py:704
